TPU v7x, 32 devices: a whole 2x2x4 slice. The times are simulated.
32 devices in a mesh: spin: 2 (over x), row: 4 (over z), col: 4 (over y, core).
Axes of the slice: x: 2, y: 2, z: 4, core: 2. Of those that a mesh axis runs over, the one named last changes fastest.
Arguments:
- hamiltonian: float32 [4096, 2048], P(('spin', 'row'), 'col'), parts along dimension 0
- bounds: float32 [4], P('spin'), parts along dimension 0
- occ_count: int32 [2], P('spin'), parts along dimension 0
- branches: int32 [12], P('spin'), parts along dimension 0
Outputs:
- output 1: float32 [4096, 2048], P(('spin', 'row'), 'col'), parts along dimension 0
- output 2: float32 [12], P('spin'), parts along dimension 0
- output 3: float32 [2], P('spin'), parts along dimension 0
There are 2 independent parts. A program takes and returns all parts, laid end to end along the dimension named above; each array names one.
All inputs are finite; a program needn't handle non-finite values.
Results may differ from a plain program's by a relative error of at most 0.001.
Values sent between devices are 32-bit elements.
A program may use at most 1 GiB of HBM per device.

v0:
```python
import jax
import jax.numpy as jnp
from jax import lax
from jax.sharding import PartitionSpec as P


def solution(mesh):
    grid_size = mesh.shape["row"]
    left_perm = [(row_pos * grid_size + (row_pos + col_pos) % grid_size, row_pos * grid_size + col_pos) for row_pos in range(grid_size) for col_pos in range(grid_size)]
    right_perm = [(((row_pos + col_pos) % grid_size) * grid_size + col_pos, row_pos * grid_size + col_pos) for row_pos in range(grid_size) for col_pos in range(grid_size)]
    shift_perm = [(src_index, (src_index - 1) % grid_size) for src_index in range(grid_size)]

    def block_product(left_block, right_block):
        return jnp.dot(left_block, right_block, preferred_element_type=jnp.float32, precision=lax.Precision.HIGHEST)

    def grid_square(local_block):
        left_block = lax.ppermute(local_block, ("row", "col"), left_perm)
        right_block = lax.ppermute(local_block, ("row", "col"), right_perm)
        partial_sum = block_product(left_block, right_block)
        for hop_index in range(grid_size - 1):
            left_block = lax.ppermute(left_block, "col", shift_perm)
            right_block = lax.ppermute(right_block, "row", shift_perm)
            partial_sum = partial_sum + block_product(left_block, right_block)
        return partial_sum

    def local_run(ham_block, bounds, occ_count, branches):
        block_size = ham_block.shape[0]
        mat_order = block_size * grid_size
        on_diag = lax.axis_index("row") == lax.axis_index("col")
        diag_mask = jnp.logical_and(jnp.arange(block_size)[:, None] == jnp.arange(block_size)[None, :], on_diag)
        chem_pot = lax.psum(jnp.where(on_diag, jnp.trace(ham_block), 0.0), ("row", "col")) / mat_order
        occupied = occ_count[0].astype(jnp.float32)
        scale_fac = jnp.minimum(occupied / (bounds[1] - chem_pot), (mat_order - occupied) / (chem_pot - bounds[0]))
        density = (scale_fac / mat_order) * (jnp.where(diag_mask, chem_pot, 0.0) - ham_block) + jnp.where(diag_mask, occupied / mat_order, 0.0)
        occ_list = []
        for step_idx in range(branches.shape[0]):
            occ_list.append(lax.psum(jnp.sum(density * density), ("row", "col")))
            squared = grid_square(density)
            density = jnp.where(branches[step_idx] == 1, squared, 2.0 * density - squared)
        energy = lax.psum(2.0 * jnp.sum(density * ham_block), ("row", "col"))
        return density, jnp.stack(occ_list), energy.reshape(1)

    return jax.shard_map(local_run, mesh=mesh, in_specs=(P(("spin", "row"), "col"), P("spin"), P("spin"), P("spin")), out_specs=(P(("spin", "row"), "col"), P("spin"), P("spin")), check_vma=False)
```

profile of v0, /device:TPU:0, one launch (start us, length us, event | category | flops | bytes accessed | tf_op | source)
XLA Modules:
  0.0 792.9 jit_solution(13278325306694306976)
XLA Ops:
  3.3 35.5 %psum.56 = f32[]{:T(128)} all-reduce(f32[]{:T(128)S(6)} %select_n.61), channel_id=1, replica_groups=mesh['spin'=2,'row'=4,'col'=4] {'row','col'}, use_global_device_ids=true, to_apply=%region_1.2 | all-reduce | flops 1 | bytes 8 | tf_op jit(solution)/shard_map/psum | solution.py:31
  44.8 12.9 %collective-permute-start.3 = (f32[512,512]{1,0:T(8,128)S(1)}, f32[512,512]{1,0:T(8,128)S(1)}, u32[]{:S(2)}, u32[]{:S(2)}) collective-permute-start(f32[512,512]{1,0:T(8,128)S(1)} %collective-permute-done.1), channel_id=1, source_target_pairs={{0,12},{4,0},{8,4},{12,8},{1,13},{5,1},{9,5},{13,9},{2,14},{6,2},{... | collective-permute-start | bytes 3145736 | tf_op jit(solution)/shard_map/ppermute | solution.py:22
  57.6 11.9 %collective-permute-start.4 = (f32[512,512]{1,0:T(8,128)S(1)}, f32[512,512]{1,0:T(8,128)S(1)}, u32[]{:S(2)}, u32[]{:S(2)}) collective-permute-start(f32[512,512]{1,0:T(8,128)S(1)} %collective-permute-done.2), channel_id=1, source_target_pairs={{0,3},{1,0},{2,1},{3,2},{4,7},{5,4},{6,5},{7,6},{8,11},{9,8},{10,9... | collective-permute-start | bytes 3145736 | tf_op jit(solution)/shard_map/ppermute | solution.py:21
  69.6 10.0 %collective-permute-done.3 = f32[512,512]{1,0:T(8,128)S(1)} collective-permute-done((f32[512,512]{1,0:T(8,128)S(1)}, f32[512,512]{1,0:T(8,128)S(1)}, u32[]{:S(2)}, u32[]{:S(2)}) %collective-permute-start.3) | collective-permute-done | bytes 1048608 | tf_op jit(solution)/shard_map/ppermute | solution.py:22
  93.3 15.5 %collective-permute-done.5 = f32[512,512]{1,0:T(8,128)S(1)} collective-permute-done((f32[512,512]{1,0:T(8,128)S(1)}, f32[512,512]{1,0:T(8,128)S(1)}, u32[]{:S(2)}, u32[]{:S(2)}) %collective-permute-start.5) | collective-permute-done | bytes 1048608 | tf_op jit(solution)/shard_map/ppermute | solution.py:22
  120.1 14.5 %collective-permute-done.7 = f32[512,512]{1,0:T(8,128)S(1)} collective-permute-done((f32[512,512]{1,0:T(8,128)S(1)}, f32[512,512]{1,0:T(8,128)S(1)}, u32[]{:S(2)}, u32[]{:S(2)}) %collective-permute-start.7) | collective-permute-done | bytes 1048608 | tf_op jit(solution)/shard_map/ppermute | solution.py:22
  138.9 25.7 %collective-permute-start.10 = (f32[512,512]{1,0:T(8,128)S(1)}, f32[512,512]{1,0:T(8,128)S(1)}, u32[]{:S(2)}, u32[]{:S(2)}) collective-permute-start(f32[512,512]{1,0:T(8,128)S(1)} %collective-permute-done.8), channel_id=1, source_target_pairs={{0,3},{1,0},{2,1},{3,2},{4,7},{5,4},{6,5},{7,6},{8,11},{9,8},{10,9... | collective-permute-start | bytes 3145736 | tf_op jit(solution)/shard_map/ppermute | solution.py:21
  176.9 12.2 %collective-permute-start.12 = (f32[512,512]{1,0:T(8,128)S(1)}, f32[512,512]{1,0:T(8,128)S(1)}, u32[]{:S(2)}, u32[]{:S(2)}) collective-permute-start(f32[512,512]{1,0:T(8,128)S(1)} %collective-permute-done.10), channel_id=1, source_target_pairs={{0,3},{1,0},{2,1},{3,2},{4,7},{5,4},{6,5},{7,6},{8,11},{9,8},{10,9... | collective-permute-start | bytes 3145736 | tf_op jit(solution)/shard_map/ppermute | solution.py:21
  191.7 16.4 %collective-permute-start.13 = (f32[512,512]{1,0:T(8,128)S(1)}, f32[512,512]{1,0:T(8,128)S(1)}, u32[]{:S(2)}, u32[]{:S(2)}) collective-permute-start(f32[512,512]{1,0:T(8,128)S(1)} %collective-permute-done.11), channel_id=1, source_target_pairs={{0,12},{4,0},{8,4},{12,8},{1,13},{5,1},{9,5},{13,9},{2,14},{6,2},{... | collective-permute-start | bytes 3145736 | tf_op jit(solution)/shard_map/ppermute | solution.py:22
  208.0 17.0 %collective-permute-start.14 = (f32[512,512]{1,0:T(8,128)S(1)}, f32[512,512]{1,0:T(8,128)S(1)}, u32[]{:S(2)}, u32[]{:S(2)}) collective-permute-start(f32[512,512]{1,0:T(8,128)S(1)} %collective-permute-done.12), channel_id=1, source_target_pairs={{0,3},{1,0},{2,1},{3,2},{4,7},{5,4},{6,5},{7,6},{8,11},{9,8},{10,9... | collective-permute-start | bytes 3145736 | tf_op jit(solution)/shard_map/ppermute | solution.py:21
  241.7 17.2 %collective-permute-done.15 = f32[512,512]{1,0:T(8,128)S(1)} collective-permute-done((f32[512,512]{1,0:T(8,128)S(1)}, f32[512,512]{1,0:T(8,128)S(1)}, u32[]{:S(2)}, u32[]{:S(2)}) %collective-permute-start.15) | collective-permute-done | bytes 1048608 | tf_op jit(solution)/shard_map/ppermute | solution.py:22
  263.1 19.4 %collective-permute-start.18 = (f32[512,512]{1,0:T(8,128)S(1)}, f32[512,512]{1,0:T(8,128)S(1)}, u32[]{:S(2)}, u32[]{:S(2)}) collective-permute-start(f32[512,512]{1,0:T(8,128)S(1)} %collective-permute-done.16), channel_id=1, source_target_pairs={{0,3},{1,0},{2,1},{3,2},{4,7},{5,4},{6,5},{7,6},{8,11},{9,8},{10,9... | collective-permute-start | bytes 3145736 | tf_op jit(solution)/shard_map/ppermute | solution.py:21
  285.6 9.1 %collective-permute-done.18 = f32[512,512]{1,0:T(8,128)S(1)} collective-permute-done((f32[512,512]{1,0:T(8,128)S(1)}, f32[512,512]{1,0:T(8,128)S(1)}, u32[]{:S(2)}, u32[]{:S(2)}) %collective-permute-start.18) | collective-permute-done | bytes 1048608 | tf_op jit(solution)/shard_map/ppermute | solution.py:21
  306.8 22.1 %collective-permute-start.21 = (f32[512,512]{1,0:T(8,128)S(1)}, f32[512,512]{1,0:T(8,128)S(1)}, u32[]{:S(2)}, u32[]{:S(2)}) collective-permute-start(f32[512,512]{1,0:T(8,128)S(1)} %collective-permute-done.19), channel_id=1, source_target_pairs={{0,12},{4,0},{8,4},{12,8},{1,13},{5,1},{9,5},{13,9},{2,14},{6,2},{... | collective-permute-start | bytes 3145736 | tf_op jit(solution)/shard_map/ppermute | solution.py:22
  328.9 19.9 %collective-permute-start.22 = (f32[512,512]{1,0:T(8,128)S(1)}, f32[512,512]{1,0:T(8,128)S(1)}, u32[]{:S(2)}, u32[]{:S(2)}) collective-permute-start(f32[512,512]{1,0:T(8,128)S(1)} %collective-permute-done.20), channel_id=1, source_target_pairs={{0,3},{1,0},{2,1},{3,2},{4,7},{5,4},{6,5},{7,6},{8,11},{9,8},{10,9... | collective-permute-start | bytes 3145736 | tf_op jit(solution)/shard_map/ppermute | solution.py:21
  361.1 9.0 %collective-permute-done.23 = f32[512,512]{1,0:T(8,128)S(1)} collective-permute-done((f32[512,512]{1,0:T(8,128)S(1)}, f32[512,512]{1,0:T(8,128)S(1)}, u32[]{:S(2)}, u32[]{:S(2)}) %collective-permute-start.23) | collective-permute-done | bytes 1048608 | tf_op jit(solution)/shard_map/ppermute | solution.py:22
  374.3 29.2 %collective-permute-start.26 = (f32[512,512]{1,0:T(8,128)S(1)}, f32[512,512]{1,0:T(8,128)S(1)}, u32[]{:S(2)}, u32[]{:S(2)}) collective-permute-start(f32[512,512]{1,0:T(8,128)S(1)} %collective-permute-done.24), channel_id=1, source_target_pairs={{0,3},{1,0},{2,1},{3,2},{4,7},{5,4},{6,5},{7,6},{8,11},{9,8},{10,9... | collective-permute-start | bytes 3145736 | tf_op jit(solution)/shard_map/ppermute | solution.py:21
  415.9 9.1 %collective-permute-start.28 = (f32[512,512]{1,0:T(8,128)S(1)}, f32[512,512]{1,0:T(8,128)S(1)}, u32[]{:S(2)}, u32[]{:S(2)}) collective-permute-start(f32[512,512]{1,0:T(8,128)S(1)} %collective-permute-done.26), channel_id=1, source_target_pairs={{0,3},{1,0},{2,1},{3,2},{4,7},{5,4},{6,5},{7,6},{8,11},{9,8},{10,9... | collective-permute-start | bytes 3145736 | tf_op jit(solution)/shard_map/ppermute | solution.py:21
  432.0 16.5 %collective-permute-start.29 = (f32[512,512]{1,0:T(8,128)S(1)}, f32[512,512]{1,0:T(8,128)S(1)}, u32[]{:S(2)}, u32[]{:S(2)}) collective-permute-start(f32[512,512]{1,0:T(8,128)S(1)} %collective-permute-done.27), channel_id=1, source_target_pairs={{0,12},{4,0},{8,4},{12,8},{1,13},{5,1},{9,5},{13,9},{2,14},{6,2},{... | collective-permute-start | bytes 3145736 | tf_op jit(solution)/shard_map/ppermute | solution.py:22
  448.5 18.3 %collective-permute-start.30 = (f32[512,512]{1,0:T(8,128)S(1)}, f32[512,512]{1,0:T(8,128)S(1)}, u32[]{:S(2)}, u32[]{:S(2)}) collective-permute-start(f32[512,512]{1,0:T(8,128)S(1)} %collective-permute-done.28), channel_id=1, source_target_pairs={{0,3},{1,0},{2,1},{3,2},{4,7},{5,4},{6,5},{7,6},{8,11},{9,8},{10,9... | collective-permute-start | bytes 3145736 | tf_op jit(solution)/shard_map/ppermute | solution.py:21
  480.6 14.0 %collective-permute-done.31 = f32[512,512]{1,0:T(8,128)S(1)} collective-permute-done((f32[512,512]{1,0:T(8,128)S(1)}, f32[512,512]{1,0:T(8,128)S(1)}, u32[]{:S(2)}, u32[]{:S(2)}) %collective-permute-start.31) | collective-permute-done | bytes 1048608 | tf_op jit(solution)/shard_map/ppermute | solution.py:22
  498.7 24.2 %collective-permute-start.34 = (f32[512,512]{1,0:T(8,128)S(1)}, f32[512,512]{1,0:T(8,128)S(1)}, u32[]{:S(2)}, u32[]{:S(2)}) collective-permute-start(f32[512,512]{1,0:T(8,128)S(1)} %collective-permute-done.32), channel_id=1, source_target_pairs={{0,3},{1,0},{2,1},{3,2},{4,7},{5,4},{6,5},{7,6},{8,11},{9,8},{10,9... | collective-permute-start | bytes 3145736 | tf_op jit(solution)/shard_map/ppermute | solution.py:21
  535.2 8.9 %collective-permute-start.36 = (f32[512,512]{1,0:T(8,128)S(1)}, f32[512,512]{1,0:T(8,128)S(1)}, u32[]{:S(2)}, u32[]{:S(2)}) collective-permute-start(f32[512,512]{1,0:T(8,128)S(1)} %collective-permute-done.34), channel_id=1, source_target_pairs={{0,3},{1,0},{2,1},{3,2},{4,7},{5,4},{6,5},{7,6},{8,11},{9,8},{10,9... | collective-permute-start | bytes 3145736 | tf_op jit(solution)/shard_map/ppermute | solution.py:21
  548.5 19.9 %collective-permute-start.37 = (f32[512,512]{1,0:T(8,128)S(1)}, f32[512,512]{1,0:T(8,128)S(1)}, u32[]{:S(2)}, u32[]{:S(2)}) collective-permute-start(f32[512,512]{1,0:T(8,128)S(1)} %collective-permute-done.35), channel_id=1, source_target_pairs={{0,12},{4,0},{8,4},{12,8},{1,13},{5,1},{9,5},{13,9},{2,14},{6,2},{... | collective-permute-start | bytes 3145736 | tf_op jit(solution)/shard_map/ppermute | solution.py:22
  568.4 18.9 %collective-permute-start.38 = (f32[512,512]{1,0:T(8,128)S(1)}, f32[512,512]{1,0:T(8,128)S(1)}, u32[]{:S(2)}, u32[]{:S(2)}) collective-permute-start(f32[512,512]{1,0:T(8,128)S(1)} %collective-permute-done.36), channel_id=1, source_target_pairs={{0,3},{1,0},{2,1},{3,2},{4,7},{5,4},{6,5},{7,6},{8,11},{9,8},{10,9... | collective-permute-start | bytes 3145736 | tf_op jit(solution)/shard_map/ppermute | solution.py:21
  599.6 11.9 %collective-permute-done.39 = f32[512,512]{1,0:T(8,128)S(1)} collective-permute-done((f32[512,512]{1,0:T(8,128)S(1)}, f32[512,512]{1,0:T(8,128)S(1)}, u32[]{:S(2)}, u32[]{:S(2)}) %collective-permute-start.39) | collective-permute-done | bytes 1048608 | tf_op jit(solution)/shard_map/ppermute | solution.py:22
  615.7 27.2 %collective-permute-start.42 = (f32[512,512]{1,0:T(8,128)S(1)}, f32[512,512]{1,0:T(8,128)S(1)}, u32[]{:S(2)}, u32[]{:S(2)}) collective-permute-start(f32[512,512]{1,0:T(8,128)S(1)} %collective-permute-done.40), channel_id=1, source_target_pairs={{0,3},{1,0},{2,1},{3,2},{4,7},{5,4},{6,5},{7,6},{8,11},{9,8},{10,9... | collective-permute-start | bytes 3145736 | tf_op jit(solution)/shard_map/ppermute | solution.py:21
  655.1 8.9 %collective-permute-start.44 = (f32[512,512]{1,0:T(8,128)S(1)}, f32[512,512]{1,0:T(8,128)S(1)}, u32[]{:S(2)}, u32[]{:S(2)}) collective-permute-start(f32[512,512]{1,0:T(8,128)S(1)} %collective-permute-done.42), channel_id=1, source_target_pairs={{0,3},{1,0},{2,1},{3,2},{4,7},{5,4},{6,5},{7,6},{8,11},{9,8},{10,9... | collective-permute-start | bytes 3145736 | tf_op jit(solution)/shard_map/ppermute | solution.py:21
  669.1 19.0 %collective-permute-start.45 = (f32[512,512]{1,0:T(8,128)S(1)}, f32[512,512]{1,0:T(8,128)S(1)}, u32[]{:S(2)}, u32[]{:S(2)}) collective-permute-start(f32[512,512]{1,0:T(8,128)S(1)} %collective-permute-done.43), channel_id=1, source_target_pairs={{0,12},{4,0},{8,4},{12,8},{1,13},{5,1},{9,5},{13,9},{2,14},{6,2},{... | collective-permute-start | bytes 3145736 | tf_op jit(solution)/shard_map/ppermute | solution.py:22
  688.1 18.7 %collective-permute-start.46 = (f32[512,512]{1,0:T(8,128)S(1)}, f32[512,512]{1,0:T(8,128)S(1)}, u32[]{:S(2)}, u32[]{:S(2)}) collective-permute-start(f32[512,512]{1,0:T(8,128)S(1)} %collective-permute-done.44), channel_id=1, source_target_pairs={{0,3},{1,0},{2,1},{3,2},{4,7},{5,4},{6,5},{7,6},{8,11},{9,8},{10,9... | collective-permute-start | bytes 3145736 | tf_op jit(solution)/shard_map/ppermute | solution.py:21
  719.2 12.9 %collective-permute-done.47 = f32[512,512]{1,0:T(8,128)S(1)} collective-permute-done((f32[512,512]{1,0:T(8,128)S(1)}, f32[512,512]{1,0:T(8,128)S(1)}, u32[]{:S(2)}, u32[]{:S(2)}) %collective-permute-start.47) | collective-permute-done | bytes 1048608 | tf_op jit(solution)/shard_map/ppermute | solution.py:22
  736.3 51.7 %all-reduce = (f32[1]{0:T(128)}, f32[1]{0:T(128)}, f32[1]{0:T(128)}, f32[1]{0:T(128)}, f32[1]{0:T(128)}, /*index=5*/f32[1]{0:T(128)}, f32[1]{0:T(128)}) all-reduce(f32[1]{0:T(128)} %bitcast.9, f32[1]{0:T(128)} %bitcast.10, f32[1]{0:T(128)} %bitcast.11, f32[1]{0:T(128)} %bitcast.12, ...), channel_id=1, replica_groups=mesh['spin'=2,'row'=4,'col'=4] {'row','col'}, use_global_device_ids=true, to_apply=%region_3.4 | all-reduce | flops 7 | bytes 56 | tf_op jit(solution)/shard_map/psum | solution.py:37
  (101 shorter events, 205.9 us)
Async XLA Ops:
  44.8 34.8 %collective-permute-start.3 = (f32[512,512]{1,0:T(8,128)S(1)}, f32[512,512]{1,0:T(8,128)S(1)}, u32[]{:S(2)}, u32[]{:S(2)}) collective-permute-start(f32[512,512]{1,0:T(8,128)S(1)} %collective-permute-done.1), channel_id=1, source_target_pairs={{0,12},{4,0},{8,4},{12,8},{1,13},{5,1},{9,5},{13,9},{2,14},{6,2},{... | collective-permute-start | bytes 3145736 | tf_op jit(solution)/shard_map/ppermute | solution.py:22
  57.6 28.4 %collective-permute-start.4 = (f32[512,512]{1,0:T(8,128)S(1)}, f32[512,512]{1,0:T(8,128)S(1)}, u32[]{:S(2)}, u32[]{:S(2)}) collective-permute-start(f32[512,512]{1,0:T(8,128)S(1)} %collective-permute-done.2), channel_id=1, source_target_pairs={{0,3},{1,0},{2,1},{3,2},{4,7},{5,4},{6,5},{7,6},{8,11},{9,8},{10,9... | collective-permute-start | bytes 3145736 | tf_op jit(solution)/shard_map/ppermute | solution.py:21
  79.6 29.3 %collective-permute-start.5 = (f32[512,512]{1,0:T(8,128)S(1)}, f32[512,512]{1,0:T(8,128)S(1)}, u32[]{:S(2)}, u32[]{:S(2)}) collective-permute-start(f32[512,512]{1,0:T(8,128)S(1)} %collective-permute-done.3), channel_id=1, source_target_pairs={{0,12},{4,0},{8,4},{12,8},{1,13},{5,1},{9,5},{13,9},{2,14},{6,2},{... | collective-permute-start | bytes 3145736 | tf_op jit(solution)/shard_map/ppermute | solution.py:22
  86.0 34.1 %collective-permute-start.6 = (f32[512,512]{1,0:T(8,128)S(1)}, f32[512,512]{1,0:T(8,128)S(1)}, u32[]{:S(2)}, u32[]{:S(2)}) collective-permute-start(f32[512,512]{1,0:T(8,128)S(1)} %collective-permute-done.4), channel_id=1, source_target_pairs={{0,3},{1,0},{2,1},{3,2},{4,7},{5,4},{6,5},{7,6},{8,11},{9,8},{10,9... | collective-permute-start | bytes 3145736 | tf_op jit(solution)/shard_map/ppermute | solution.py:21
  108.8 25.8 %collective-permute-start.7 = (f32[512,512]{1,0:T(8,128)S(1)}, f32[512,512]{1,0:T(8,128)S(1)}, u32[]{:S(2)}, u32[]{:S(2)}) collective-permute-start(f32[512,512]{1,0:T(8,128)S(1)} %collective-permute-done.5), channel_id=1, source_target_pairs={{0,12},{4,0},{8,4},{12,8},{1,13},{5,1},{9,5},{13,9},{2,14},{6,2},{... | collective-permute-start | bytes 3145736 | tf_op jit(solution)/shard_map/ppermute | solution.py:22
  138.1 26.5 %collective-permute-start.9 = (f32[512,512]{1,0:T(8,128)S(1)}, f32[512,512]{1,0:T(8,128)S(1)}, u32[]{:S(2)}, u32[]{:S(2)}) collective-permute-start(f32[512,512]{1,0:T(8,128)S(1)} %get-tuple-element.21), channel_id=1, source_target_pairs={{0,0},{5,1},{10,2},{15,3},{4,4},{9,5},{14,6},{3,7},{8,8},{13,9},{2... | collective-permute-start | bytes 3145736 | tf_op jit(solution)/shard_map/ppermute | solution.py:18
  138.9 38.0 %collective-permute-start.10 = (f32[512,512]{1,0:T(8,128)S(1)}, f32[512,512]{1,0:T(8,128)S(1)}, u32[]{:S(2)}, u32[]{:S(2)}) collective-permute-start(f32[512,512]{1,0:T(8,128)S(1)} %collective-permute-done.8), channel_id=1, source_target_pairs={{0,3},{1,0},{2,1},{3,2},{4,7},{5,4},{6,5},{7,6},{8,11},{9,8},{10,9... | collective-permute-start | bytes 3145736 | tf_op jit(solution)/shard_map/ppermute | solution.py:21
  164.6 27.1 %collective-permute-start.11 = (f32[512,512]{1,0:T(8,128)S(1)}, f32[512,512]{1,0:T(8,128)S(1)}, u32[]{:S(2)}, u32[]{:S(2)}) collective-permute-start(f32[512,512]{1,0:T(8,128)S(1)} %collective-permute-done.9), channel_id=1, source_target_pairs={{0,12},{4,0},{8,4},{12,8},{1,13},{5,1},{9,5},{13,9},{2,14},{6,2},{... | collective-permute-start | bytes 3145736 | tf_op jit(solution)/shard_map/ppermute | solution.py:22
  176.9 31.2 %collective-permute-start.12 = (f32[512,512]{1,0:T(8,128)S(1)}, f32[512,512]{1,0:T(8,128)S(1)}, u32[]{:S(2)}, u32[]{:S(2)}) collective-permute-start(f32[512,512]{1,0:T(8,128)S(1)} %collective-permute-done.10), channel_id=1, source_target_pairs={{0,3},{1,0},{2,1},{3,2},{4,7},{5,4},{6,5},{7,6},{8,11},{9,8},{10,9... | collective-permute-start | bytes 3145736 | tf_op jit(solution)/shard_map/ppermute | solution.py:21
  191.7 39.0 %collective-permute-start.13 = (f32[512,512]{1,0:T(8,128)S(1)}, f32[512,512]{1,0:T(8,128)S(1)}, u32[]{:S(2)}, u32[]{:S(2)}) collective-permute-start(f32[512,512]{1,0:T(8,128)S(1)} %collective-permute-done.11), channel_id=1, source_target_pairs={{0,12},{4,0},{8,4},{12,8},{1,13},{5,1},{9,5},{13,9},{2,14},{6,2},{... | collective-permute-start | bytes 3145736 | tf_op jit(solution)/shard_map/ppermute | solution.py:22
  208.0 33.7 %collective-permute-start.14 = (f32[512,512]{1,0:T(8,128)S(1)}, f32[512,512]{1,0:T(8,128)S(1)}, u32[]{:S(2)}, u32[]{:S(2)}) collective-permute-start(f32[512,512]{1,0:T(8,128)S(1)} %collective-permute-done.12), channel_id=1, source_target_pairs={{0,3},{1,0},{2,1},{3,2},{4,7},{5,4},{6,5},{7,6},{8,11},{9,8},{10,9... | collective-permute-start | bytes 3145736 | tf_op jit(solution)/shard_map/ppermute | solution.py:21
  230.7 28.2 %collective-permute-start.15 = (f32[512,512]{1,0:T(8,128)S(1)}, f32[512,512]{1,0:T(8,128)S(1)}, u32[]{:S(2)}, u32[]{:S(2)}) collective-permute-start(f32[512,512]{1,0:T(8,128)S(1)} %collective-permute-done.13), channel_id=1, source_target_pairs={{0,12},{4,0},{8,4},{12,8},{1,13},{5,1},{9,5},{13,9},{2,14},{6,2},{... | collective-permute-start | bytes 3145736 | tf_op jit(solution)/shard_map/ppermute | solution.py:22
  263.1 31.7 %collective-permute-start.18 = (f32[512,512]{1,0:T(8,128)S(1)}, f32[512,512]{1,0:T(8,128)S(1)}, u32[]{:S(2)}, u32[]{:S(2)}) collective-permute-start(f32[512,512]{1,0:T(8,128)S(1)} %collective-permute-done.16), channel_id=1, source_target_pairs={{0,3},{1,0},{2,1},{3,2},{4,7},{5,4},{6,5},{7,6},{8,11},{9,8},{10,9... | collective-permute-start | bytes 3145736 | tf_op jit(solution)/shard_map/ppermute | solution.py:21
  294.8 34.2 %collective-permute-start.20 = (f32[512,512]{1,0:T(8,128)S(1)}, f32[512,512]{1,0:T(8,128)S(1)}, u32[]{:S(2)}, u32[]{:S(2)}) collective-permute-start(f32[512,512]{1,0:T(8,128)S(1)} %collective-permute-done.18), channel_id=1, source_target_pairs={{0,3},{1,0},{2,1},{3,2},{4,7},{5,4},{6,5},{7,6},{8,11},{9,8},{10,9... | collective-permute-start | bytes 3145736 | tf_op jit(solution)/shard_map/ppermute | solution.py:21
  306.8 42.0 %collective-permute-start.21 = (f32[512,512]{1,0:T(8,128)S(1)}, f32[512,512]{1,0:T(8,128)S(1)}, u32[]{:S(2)}, u32[]{:S(2)}) collective-permute-start(f32[512,512]{1,0:T(8,128)S(1)} %collective-permute-done.19), channel_id=1, source_target_pairs={{0,12},{4,0},{8,4},{12,8},{1,13},{5,1},{9,5},{13,9},{2,14},{6,2},{... | collective-permute-start | bytes 3145736 | tf_op jit(solution)/shard_map/ppermute | solution.py:22
  328.9 32.2 %collective-permute-start.22 = (f32[512,512]{1,0:T(8,128)S(1)}, f32[512,512]{1,0:T(8,128)S(1)}, u32[]{:S(2)}, u32[]{:S(2)}) collective-permute-start(f32[512,512]{1,0:T(8,128)S(1)} %collective-permute-done.20), channel_id=1, source_target_pairs={{0,3},{1,0},{2,1},{3,2},{4,7},{5,4},{6,5},{7,6},{8,11},{9,8},{10,9... | collective-permute-start | bytes 3145736 | tf_op jit(solution)/shard_map/ppermute | solution.py:21
  373.6 30.0 %collective-permute-start.25 = (f32[512,512]{1,0:T(8,128)S(1)}, f32[512,512]{1,0:T(8,128)S(1)}, u32[]{:S(2)}, u32[]{:S(2)}) collective-permute-start(f32[512,512]{1,0:T(8,128)S(1)} %get-tuple-element.25), channel_id=1, source_target_pairs={{0,0},{5,1},{10,2},{15,3},{4,4},{9,5},{14,6},{3,7},{8,8},{13,9},{2... | collective-permute-start | bytes 3145736 | tf_op jit(solution)/shard_map/ppermute | solution.py:18
  374.3 41.5 %collective-permute-start.26 = (f32[512,512]{1,0:T(8,128)S(1)}, f32[512,512]{1,0:T(8,128)S(1)}, u32[]{:S(2)}, u32[]{:S(2)}) collective-permute-start(f32[512,512]{1,0:T(8,128)S(1)} %collective-permute-done.24), channel_id=1, source_target_pairs={{0,3},{1,0},{2,1},{3,2},{4,7},{5,4},{6,5},{7,6},{8,11},{9,8},{10,9... | collective-permute-start | bytes 3145736 | tf_op jit(solution)/shard_map/ppermute | solution.py:21
  403.6 28.4 %collective-permute-start.27 = (f32[512,512]{1,0:T(8,128)S(1)}, f32[512,512]{1,0:T(8,128)S(1)}, u32[]{:S(2)}, u32[]{:S(2)}) collective-permute-start(f32[512,512]{1,0:T(8,128)S(1)} %collective-permute-done.25), channel_id=1, source_target_pairs={{0,12},{4,0},{8,4},{12,8},{1,13},{5,1},{9,5},{13,9},{2,14},{6,2},{... | collective-permute-start | bytes 3145736 | tf_op jit(solution)/shard_map/ppermute | solution.py:22
  415.9 32.6 %collective-permute-start.28 = (f32[512,512]{1,0:T(8,128)S(1)}, f32[512,512]{1,0:T(8,128)S(1)}, u32[]{:S(2)}, u32[]{:S(2)}) collective-permute-start(f32[512,512]{1,0:T(8,128)S(1)} %collective-permute-done.26), channel_id=1, source_target_pairs={{0,3},{1,0},{2,1},{3,2},{4,7},{5,4},{6,5},{7,6},{8,11},{9,8},{10,9... | collective-permute-start | bytes 3145736 | tf_op jit(solution)/shard_map/ppermute | solution.py:21
  432.0 38.0 %collective-permute-start.29 = (f32[512,512]{1,0:T(8,128)S(1)}, f32[512,512]{1,0:T(8,128)S(1)}, u32[]{:S(2)}, u32[]{:S(2)}) collective-permute-start(f32[512,512]{1,0:T(8,128)S(1)} %collective-permute-done.27), channel_id=1, source_target_pairs={{0,12},{4,0},{8,4},{12,8},{1,13},{5,1},{9,5},{13,9},{2,14},{6,2},{... | collective-permute-start | bytes 3145736 | tf_op jit(solution)/shard_map/ppermute | solution.py:22
  448.5 32.1 %collective-permute-start.30 = (f32[512,512]{1,0:T(8,128)S(1)}, f32[512,512]{1,0:T(8,128)S(1)}, u32[]{:S(2)}, u32[]{:S(2)}) collective-permute-start(f32[512,512]{1,0:T(8,128)S(1)} %collective-permute-done.28), channel_id=1, source_target_pairs={{0,3},{1,0},{2,1},{3,2},{4,7},{5,4},{6,5},{7,6},{8,11},{9,8},{10,9... | collective-permute-start | bytes 3145736 | tf_op jit(solution)/shard_map/ppermute | solution.py:21
  498.7 36.5 %collective-permute-start.34 = (f32[512,512]{1,0:T(8,128)S(1)}, f32[512,512]{1,0:T(8,128)S(1)}, u32[]{:S(2)}, u32[]{:S(2)}) collective-permute-start(f32[512,512]{1,0:T(8,128)S(1)} %collective-permute-done.32), channel_id=1, source_target_pairs={{0,3},{1,0},{2,1},{3,2},{4,7},{5,4},{6,5},{7,6},{8,11},{9,8},{10,9... | collective-permute-start | bytes 3145736 | tf_op jit(solution)/shard_map/ppermute | solution.py:21
  535.2 33.2 %collective-permute-start.36 = (f32[512,512]{1,0:T(8,128)S(1)}, f32[512,512]{1,0:T(8,128)S(1)}, u32[]{:S(2)}, u32[]{:S(2)}) collective-permute-start(f32[512,512]{1,0:T(8,128)S(1)} %collective-permute-done.34), channel_id=1, source_target_pairs={{0,3},{1,0},{2,1},{3,2},{4,7},{5,4},{6,5},{7,6},{8,11},{9,8},{10,9... | collective-permute-start | bytes 3145736 | tf_op jit(solution)/shard_map/ppermute | solution.py:21
  548.5 39.8 %collective-permute-start.37 = (f32[512,512]{1,0:T(8,128)S(1)}, f32[512,512]{1,0:T(8,128)S(1)}, u32[]{:S(2)}, u32[]{:S(2)}) collective-permute-start(f32[512,512]{1,0:T(8,128)S(1)} %collective-permute-done.35), channel_id=1, source_target_pairs={{0,12},{4,0},{8,4},{12,8},{1,13},{5,1},{9,5},{13,9},{2,14},{6,2},{... | collective-permute-start | bytes 3145736 | tf_op jit(solution)/shard_map/ppermute | solution.py:22
  568.4 31.2 %collective-permute-start.38 = (f32[512,512]{1,0:T(8,128)S(1)}, f32[512,512]{1,0:T(8,128)S(1)}, u32[]{:S(2)}, u32[]{:S(2)}) collective-permute-start(f32[512,512]{1,0:T(8,128)S(1)} %collective-permute-done.36), channel_id=1, source_target_pairs={{0,3},{1,0},{2,1},{3,2},{4,7},{5,4},{6,5},{7,6},{8,11},{9,8},{10,9... | collective-permute-start | bytes 3145736 | tf_op jit(solution)/shard_map/ppermute | solution.py:21
  614.9 27.9 %collective-permute-start.41 = (f32[512,512]{1,0:T(8,128)S(1)}, f32[512,512]{1,0:T(8,128)S(1)}, u32[]{:S(2)}, u32[]{:S(2)}) collective-permute-start(f32[512,512]{1,0:T(8,128)S(1)} %get-tuple-element.29), channel_id=1, source_target_pairs={{0,0},{5,1},{10,2},{15,3},{4,4},{9,5},{14,6},{3,7},{8,8},{13,9},{2... | collective-permute-start | bytes 3145736 | tf_op jit(solution)/shard_map/ppermute | solution.py:18
  615.7 39.5 %collective-permute-start.42 = (f32[512,512]{1,0:T(8,128)S(1)}, f32[512,512]{1,0:T(8,128)S(1)}, u32[]{:S(2)}, u32[]{:S(2)}) collective-permute-start(f32[512,512]{1,0:T(8,128)S(1)} %collective-permute-done.40), channel_id=1, source_target_pairs={{0,3},{1,0},{2,1},{3,2},{4,7},{5,4},{6,5},{7,6},{8,11},{9,8},{10,9... | collective-permute-start | bytes 3145736 | tf_op jit(solution)/shard_map/ppermute | solution.py:21
  642.8 26.3 %collective-permute-start.43 = (f32[512,512]{1,0:T(8,128)S(1)}, f32[512,512]{1,0:T(8,128)S(1)}, u32[]{:S(2)}, u32[]{:S(2)}) collective-permute-start(f32[512,512]{1,0:T(8,128)S(1)} %collective-permute-done.41), channel_id=1, source_target_pairs={{0,12},{4,0},{8,4},{12,8},{1,13},{5,1},{9,5},{13,9},{2,14},{6,2},{... | collective-permute-start | bytes 3145736 | tf_op jit(solution)/shard_map/ppermute | solution.py:22
  655.1 32.9 %collective-permute-start.44 = (f32[512,512]{1,0:T(8,128)S(1)}, f32[512,512]{1,0:T(8,128)S(1)}, u32[]{:S(2)}, u32[]{:S(2)}) collective-permute-start(f32[512,512]{1,0:T(8,128)S(1)} %collective-permute-done.42), channel_id=1, source_target_pairs={{0,3},{1,0},{2,1},{3,2},{4,7},{5,4},{6,5},{7,6},{8,11},{9,8},{10,9... | collective-permute-start | bytes 3145736 | tf_op jit(solution)/shard_map/ppermute | solution.py:21
  669.1 39.3 %collective-permute-start.45 = (f32[512,512]{1,0:T(8,128)S(1)}, f32[512,512]{1,0:T(8,128)S(1)}, u32[]{:S(2)}, u32[]{:S(2)}) collective-permute-start(f32[512,512]{1,0:T(8,128)S(1)} %collective-permute-done.43), channel_id=1, source_target_pairs={{0,12},{4,0},{8,4},{12,8},{1,13},{5,1},{9,5},{13,9},{2,14},{6,2},{... | collective-permute-start | bytes 3145736 | tf_op jit(solution)/shard_map/ppermute | solution.py:22
  688.1 31.1 %collective-permute-start.46 = (f32[512,512]{1,0:T(8,128)S(1)}, f32[512,512]{1,0:T(8,128)S(1)}, u32[]{:S(2)}, u32[]{:S(2)}) collective-permute-start(f32[512,512]{1,0:T(8,128)S(1)} %collective-permute-done.44), channel_id=1, source_target_pairs={{0,3},{1,0},{2,1},{3,2},{4,7},{5,4},{6,5},{7,6},{8,11},{9,8},{10,9... | collective-permute-start | bytes 3145736 | tf_op jit(solution)/shard_map/ppermute | solution.py:21
  (19 other events, 357.6 us)
where the time goes:
time: 800 us; the launch traced here: 793 us
  starting transfers between devices  461 us (58%)
  waiting for transfers between devices  176 us (22%)
  blocking collectives  87.2 us (11%)
  matrix products  50.5 us (6%)
  between operations  9.31 us (1%)
    ppermute x18, starting transfers between devices, grid_square(): left_block = lax.ppermute(left_block, 'col', shift_perm)  286 us
    ppermute x18, starting transfers between devices, grid_square(): right_block = lax.ppermute(right_block, 'row', shift_perm)  167 us
    ppermute x18, waiting for transfers between devices, grid_square(): right_block = lax.ppermute(right_block, 'row', shift_perm)  139 us
    psum x1, blocking collectives, local_run(): occ_list.append(lax.psum(jnp.sum(density * density), ('row', 'col')))  51.7 us
    dot_general x24, matrix products, block_product(): jnp.dot(left_block, right_block, preferred_element_type=jnp.float32, prec...  50.5 us
    ppermute x18, waiting for transfers between devices, grid_square(): left_block = lax.ppermute(left_block, 'col', shift_perm)  37 us
    psum x1, blocking collectives, local_run(): lax.psum(jnp.where(on_diag, jnp.trace(ham_block), 0.0), ('row', 'col'))  35.5 us
  transfers between devices with their start and end apart: 48, of which 24 were waited for; matrix products, arithmetic and copies ran while one was open for 4% of the time, Pallas kernels for 0%

commit v1 on v0

v1 whole, which is shorter than its diff:
```python
import functools

import jax
import jax.numpy as jnp
from jax import lax
from jax.experimental import pallas as pl
from jax.experimental.pallas import tpu as pltpu
from jax.sharding import PartitionSpec as P

ORDERS = ((0, 1, 2), (1, 2, 0), (2, 0, 1))
F32 = jnp.float32


def neighbour(dim, row, col):
    if dim == 0:
        return row + 1 - 2 * (row % 2), col
    if dim == 1:
        return 3 - row, col
    return row, (col + 2) % 4


def thirds(rows):
    first = ((rows // 3 + 7) // 8) * 8
    sizes = (first, first, rows - 2 * first)
    return sizes, (0, first, 2 * first)


def kernel(steps, h_ref, bounds_ref, occ_ref, flag_ref, dens_ref, occs_ref, energy_ref, x_ref, stage, red, g_send, g_recv, f_send,
           f_recv, i_send, i_recv, d_send, d_recv, w_send, w_recv, r_send, r_recv, credit):
    block = h_ref.shape[0]
    half = block // 2
    order = 4 * block
    sizes, starts = thirds(half)
    spin, row, col = lax.axis_index("spin"), lax.axis_index("row"), lax.axis_index("col")
    core = col % 2
    partner = (row, col + 1 - 2 * core)
    odd = (row + col // 2) % 2

    def at(start, size):
        return pl.ds(pl.multiple_of(start, 8), size)

    def lanes(start, size):
        return pl.ds(pl.multiple_of(start, min(128, size)), size)

    def remote(src, dst, send, recv, where):
        return pltpu.make_async_remote_copy(
            src_ref=src, dst_ref=dst, send_sem=send, recv_sem=recv, device_id=(spin,) + tuple(where), device_id_type=pl.DeviceIdType.MESH
        )

    others = [(dr, dc) for dr in range(4) for dc in range(4) if dr or dc]
    barrier = pltpu.get_barrier_semaphore()
    for dr, dc in others:
        pl.semaphore_signal(
            barrier, inc=1, device_id=(spin, (row + dr) % 4, (col + dc) % 4), device_id_type=pl.DeviceIdType.MESH
        )
    pl.semaphore_wait(barrier, len(others))

    def quadrant(src, which):
        if which == 0:
            return 0, half
        if which == 2:
            return half, half
        low = jnp.where(src[0] > src[1], half, 0)
        return low, low

    def guarded(src, which, run):
        if which == 2:
            pl.when(src[0] == src[1])(run)
        else:
            run()

    def region(src, which, part):
        qr, qc = quadrant(src, which)
        return x_ref.at[1, at(src[0] * block + qr + starts[part], sizes[part]), lanes(src[1] * block + qc, half)]

    def own_region(which, part):
        qr, qc = quadrant((row, col), which)
        return h_ref.at[at(qr + starts[part], sizes[part]), lanes(qc, half)]

    x_ref[1, at(row * block, block), lanes(col * block, block)] = h_ref[...]
    stage[...] = jnp.zeros_like(stage)

    def gather_index(part, slot, which):
        return (part * 7 + slot) * 3 + which

    def forward_index(part, slot, which):
        return (part * 8 + slot) * 3 + which

    held = [[(row, col)] for _ in ORDERS]
    for part in range(3):
        for which in range(3):
            n = forward_index(part, 7, which)
            guarded((row, col), which, lambda part=part, which=which, n=n: remote(
                own_region(which, part), region((row, col), which, part), f_send.at[n], f_recv.at[n], partner).start())
    for phase in range(3):
        base = (1 << phase) - 1
        for part, dims in enumerate(ORDERS):
            target = neighbour(dims[phase], row, col)
            for k, src in enumerate(held[part]):
                for which in range(3):
                    n = gather_index(part, base + k, which)
                    source = own_region(which, part) if k == 0 else region(src, which, part)
                    guarded(src, which, lambda source=source, src=src, which=which, part=part, n=n, target=target: remote(
                        source, region(src, which, part), g_send.at[n], g_recv.at[n], target).start())
        for part, dims in enumerate(ORDERS):
            target = neighbour(dims[phase], row, col)
            fresh = [neighbour(dims[phase], *src) for src in held[part]]
            for k, src in enumerate(fresh):
                for which in range(3):
                    n = gather_index(part, base + k, which)
                    m = forward_index(part, base + k, which)

                    def arrive(src=src, which=which, part=part, n=n, m=m, target=target):
                        spot = region(src, which, part)
                        remote(spot, spot, g_send.at[n], g_recv.at[n], target).wait_recv()
                        remote(spot, spot, f_send.at[m], f_recv.at[m], partner).start()

                    guarded(src, which, arrive)
            held[part] = held[part] + fresh
    for part, dims in enumerate(ORDERS):
        for slot in range(8):
            mine = held[part][(slot + 1) % 8]
            theirs = (mine[0], mine[1] + 1 - 2 * core)
            for which in range(3):
                m = forward_index(part, slot, which)

                def settle(theirs=theirs, which=which, part=part, m=m):
                    spot = region(theirs, which, part)
                    remote(spot, spot, f_send.at[m], f_recv.at[m], partner).wait_recv()

                guarded(theirs, which, settle)

                def drain(mine=mine, which=which, part=part, m=m):
                    spot = region(mine, which, part)
                    remote(spot, spot, f_send.at[m], f_recv.at[m], partner).wait_send()

                guarded(mine, which, drain)
    for phase in range(3):
        base = (1 << phase) - 1
        for part, dims in enumerate(ORDERS):
            for k, src in enumerate(held[part][: 1 << phase]):
                for which in range(3):
                    n = gather_index(part, base + k, which)

                    def drain(src=src, which=which, part=part, n=n):
                        spot = region(src, which, part)
                        remote(spot, spot, g_send.at[n], g_recv.at[n], partner).wait_send()

                    guarded(src, which, drain)

    quad_eye = lax.broadcasted_iota(jnp.int32, (half, half), 0) == lax.broadcasted_iota(jnp.int32, (half, half), 1)
    trace = jnp.zeros((half, half), F32)
    for k in range(8):
        trace = trace + x_ref[1, k * half:(k + 1) * half, k * half:(k + 1) * half]
    trace = jnp.where(quad_eye, trace, 0.0)
    chem = jnp.sum(jnp.sum(trace, axis=0, keepdims=True), axis=1, keepdims=True) / order
    occupied = jnp.full((1, 1), occ_ref[0], jnp.int32).astype(F32)
    scale = jnp.minimum(occupied / (bounds_ref[1] - chem), (order - occupied) / (chem - bounds_ref[0])) / order
    shift = occupied / order

    def convert(n, carry):
        i, j = n // 4, n % 4
        low = jnp.where(i > j, half, 0)

        def one(qr, qc):
            eye = jnp.logical_and(quad_eye, i * block + qr == j * block + qc)
            value = x_ref[1, at(i * block + qr, half), lanes(j * block + qc, half)]
            value = scale * (jnp.where(eye, chem, 0.0) - value) + jnp.where(eye, shift, 0.0)
            x_ref[0, at(i * block + qr, half), lanes(j * block + qc, half)] = value
            x_ref[0, at(j * block + qc, half), lanes(i * block + qr, half)] = value.T

        one(0, half)
        one(low, low)

        @pl.when(i == j)
        def _():
            one(half, half)

        return carry

    lax.fori_loop(0, 16, convert, 0)

    def sigma(flip, i):
        return i + flip * (3 - 2 * i)

    def piece_at(flip, who, k):
        diag = k // 2
        i = sigma(flip, diag * who)
        j = sigma(flip, diag * who + (1 - diag) * (1 + who))
        return i * block + (k % 2) * half, j * block

    def product(cur, r0, c0, height, width, flag):
        got = jnp.dot(
            x_ref[cur, at(r0, height), :], x_ref[cur, :, lanes(c0, width)], precision=lax.Precision.HIGHEST, preferred_element_type=F32
        )
        old = x_ref[cur, at(r0, height), lanes(c0, width)]
        return jnp.where(flag == 1, got, 2.0 * old - got)

    def signal_credit():
        for dim in range(3):
            pl.semaphore_signal(credit.at[dim], inc=1, device_id=(spin,) + neighbour(dim, row, col), device_id_type=pl.DeviceIdType.MESH)
        pl.semaphore_signal(credit.at[3], inc=1, device_id=(spin,) + partner, device_id_type=pl.DeviceIdType.MESH)

    def squares(cur):
        own = x_ref[cur, at(row * block, block), lanes(col * block, block)]
        return lane_sums(own * own)

    def lane_sums(value):
        total = value[:, :128]
        for k in range(1, block // 128):
            total = total + value[:, k * 128:(k + 1) * 128]
        return jnp.sum(total, axis=0, keepdims=True)

    def step(t, carry):
        cur, nxt = t % 2, 1 - t % 2
        flag = flag_ref[t]
        stage[pl.ds(t, 1), :] = squares(cur)

        def rect(r0, c0, height, width):
            return x_ref.at[nxt, at(r0, height), lanes(c0, width)]

        def to_partner(spot, n):
            return remote(spot, spot, d_send.at[n], d_recv.at[n], partner)

        def third(flip, who, k, part, width):
            r0, c0 = piece_at(flip, who, k)
            c0 = c0 if width == block else c0 + half
            return rect(r0 + starts[part], c0, sizes[part], width)

        def width_of(k):
            return half if isinstance(k, int) and k == 3 else block

        def outward(k):
            return [remote(third(odd, core, k, d, width_of(k)), third(odd, core, k, d, width_of(k)), i_send.at[k * 3 + d], i_recv.at[k * 3 + d],
                           neighbour(d, row, col)) for d in range(3)]

        def inward(k):
            return [remote(third(1 - odd, core, k, d, width_of(k)), third(1 - odd, core, k, d, width_of(k)), i_send.at[k * 3 + d],
                           i_recv.at[k * 3 + d], neighbour(d, row, col)) for d in range(3)]

        def passed(who, k):
            return [remote(third(1 - odd, who, k, d, width_of(k)), third(1 - odd, who, k, d, width_of(k)), w_send.at[k * 3 + d],
                           w_recv.at[k * 3 + d], partner) for d in range(3)]

        def local_copies(who, k, whole):
            r0, c0 = piece_at(odd, who, k)
            spots = [rect(r0, c0, half, block), rect(c0 + half, r0, half, half)] + ([rect(c0, r0, half, half)] if whole else [])
            return [to_partner(spot, k * 3 + n) for n, spot in enumerate(spots)]

        def last_quadrant(who):
            r0, c0 = piece_at(odd, who, 3)
            return to_partner(rect(r0, c0 + half, half, half), 9)

        def shared(who):
            r0, c0 = sigma(odd, who) * block, sigma(odd, 3 - who) * block
            return [to_partner(rect(r0, c0, block, block), 10), to_partner(rect(c0, r0, block, block), 11)]

        def piece(k, carry):
            r0, c0 = piece_at(odd, core, k)
            new = product(cur, r0, c0, half, block, flag)

            @pl.when(k == 0)
            def _():
                for n in range(4):
                    pl.semaphore_wait(credit.at[n], 1)

            x_ref[nxt, at(r0, half), lanes(c0, block)] = new
            x_ref[nxt, at(c0, block), lanes(r0, half)] = new.T
            for copy in outward(k):
                copy.start()
            for copy in local_copies(core, k, False):
                copy.start()

            @pl.when(k < 2)
            def _():
                local_copies(core, k, True)[2].start()

            return carry

        def relay(k):
            for arrived, onward in zip(inward(k), passed(core, k)):
                arrived.wait_recv()
                onward.start()

        lax.fori_loop(0, 3, piece, 0)
        relay(0)
        r0, c0 = piece_at(odd, core, 3)
        x_ref[nxt, at(r0, half), lanes(c0 + half, half)] = product(cur, r0, c0 + half, half, half, flag)
        for copy in outward(3):
            copy.start()
        last_quadrant(core).start()
        relay(1)
        r0, c0 = sigma(odd, core) * block, sigma(odd, 3 - core) * block
        new = product(cur, r0, c0, block, block, flag)
        x_ref[nxt, at(r0, block), lanes(c0, block)] = new
        x_ref[nxt, at(c0, block), lanes(r0, block)] = new.T
        for copy in shared(core):
            copy.start()
        relay(2)
        relay(3)

        for k in range(3):
            for copy in local_copies(1 - core, k, k < 2):
                copy.wait_recv()
        last_quadrant(1 - core).wait_recv()
        for copy in shared(1 - core):
            copy.wait_recv()
        for k in range(4):
            for copy in passed(1 - core, k):
                copy.wait_recv()

        def mirror(n, carry):
            k, who = n // 2, n % 2
            r0, c0 = piece_at(1 - odd, who, k)
            x_ref[nxt, at(c0 + half, half), lanes(r0, half)] = x_ref[nxt, at(r0, half), lanes(c0 + half, half)].T

            @pl.when(k < 2)
            def _():
                x_ref[nxt, at(c0, half), lanes(r0, half)] = x_ref[nxt, at(r0, half), lanes(c0, half)].T

            return carry

        for k in range(4):
            for copy in outward(k) + passed(core, k):
                copy.wait_send()
        for k in range(3):
            for copy in local_copies(core, k, k < 2):
                copy.wait_send()
        last_quadrant(core).wait_send()
        for copy in shared(core):
            copy.wait_send()
        lax.fori_loop(0, 6, mirror, 0)

        @pl.when(t < steps - 2)
        def _():
            signal_credit()

        return carry

    signal_credit()
    lax.fori_loop(0, steps - 1, step, 0)

    last = (steps - 1) % 2
    stage[steps - 1:steps, :] = squares(last)
    final = product(last, row * block, col * block, block, block, flag_ref[steps - 1])
    dens_ref[...] = final
    stage[steps:steps + 1, :] = lane_sums(final * h_ref[...])

    red[row * 4 + col] = stage[...]
    for n, (dr, dc) in enumerate(others):
        remote(stage, red.at[row * 4 + col], r_send.at[n], r_recv.at[n], ((row + dr) % 4, (col + dc) % 4)).start()
    for n, (dr, dc) in enumerate(others):
        spot = red.at[((row - dr) % 4) * 4 + (col - dc) % 4]
        remote(stage, spot, r_send.at[n], r_recv.at[n], partner).wait_recv()
    total = red[0]
    for n in range(1, 16):
        total = total + red[n]
    for n in range(steps):
        occs_ref[n] = jnp.sum(total[n:n + 1, :])
    energy_ref[0] = 2.0 * jnp.sum(total[steps:steps + 1, :])
    for n, (dr, dc) in enumerate(others):
        remote(stage, red.at[row * 4 + col], r_send.at[n], r_recv.at[n], ((row + dr) % 4, (col + dc) % 4)).wait_send()


def solution(mesh):
    def local_run(ham_block, bounds, occ_count, branches):
        block, steps = ham_block.shape[0], branches.shape[0]
        order = 4 * block
        dma = pltpu.SemaphoreType.DMA
        vmem = pl.BlockSpec(memory_space=pltpu.VMEM)
        smem = pl.BlockSpec(memory_space=pltpu.SMEM)
        return pl.pallas_call(
            functools.partial(kernel, steps),
            out_shape=(
                jax.ShapeDtypeStruct((block, block), F32),
                jax.ShapeDtypeStruct((steps,), F32),
                jax.ShapeDtypeStruct((1,), F32),
            ),
            in_specs=[vmem, smem, smem, smem],
            out_specs=(vmem, smem, smem),
            scratch_shapes=[
                pltpu.VMEM((2, order, order), F32),
                pltpu.VMEM((8, 128), F32),
                pltpu.VMEM((16, 8, 128), F32),
                dma((63,)), dma((63,)), dma((72,)), dma((72,)),
                dma((12,)), dma((12,)), dma((12,)), dma((12,)), dma((12,)), dma((12,)),
                dma((15,)), dma((15,)),
                pltpu.SemaphoreType.REGULAR((4,)),
            ],
            compiler_params=pltpu.CompilerParams(collective_id=0, has_side_effects=True, vmem_limit_bytes=60 * 1024 * 1024),
        )(ham_block, bounds, occ_count, branches)

    return jax.shard_map(
        local_run,
        mesh=mesh,
        in_specs=(P(("spin", "row"), "col"), P("spin"), P("spin"), P("spin")),
        out_specs=(P(("spin", "row"), "col"), P("spin"), P("spin")),
        check_vma=False,
    )
```

time: 800 us -> 292 us (0.36)
  starting transfers between devices: 461 us -> 0 us
  Pallas kernels: 0 us -> 286 us
  waiting for transfers between devices: 176 us -> 0 us
  blocking collectives: 87.2 us -> 0 us
  matrix products: 50.5 us -> 0 us
    ppermute x48 -> x0, starting transfers between devices: 461 us -> none  [the longest x18 286 us: grid_square(): left_block = lax.ppermute(left_block, 'col', shift_perm)]
    pallas_call x0 -> x1, Pallas kernels: none -> 286 us  [local_run(): pl.pallas_call(functools.partial(kernel, steps), out_shape=(jax.ShapeDtyp...]
    ppermute x48 -> x0, waiting for transfers between devices: 176 us -> none  [the longest x18 139 us: grid_square(): right_block = lax.ppermute(right_block, 'row', shift_perm)]
    psum x2 -> x0, blocking collectives: 87.2 us -> none  [the longest x1 51.7 us: local_run(): occ_list.append(lax.psum(jnp.sum(density * density), ('row', 'col')))]
    dot_general x24 -> x0, matrix products: 50.5 us -> none  [block_product(): jnp.dot(left_block, right_block, preferred_element_type=jnp.float32, prec...]
  transfers between devices with their start and end apart: 48 -> 0, of which waited for: 24 -> 0; matrix products, arithmetic and copies ran while one was open for 4% -> 0% of each run, Pallas kernels for 0% -> 0%
where the time goes in v1:
time: 292 us
  Pallas kernels  286 us (98%)
  between operations  3.05 us (1%)
    pallas_call x1, Pallas kernels, local_run(): pl.pallas_call(functools.partial(kernel, steps), out_shape=(jax.ShapeDtyp...  286 us

profile of v1, /device:TPU:0, one launch (start us, length us, event | category | flops | bytes accessed | tf_op | source)
XLA Modules:
  0.0 291.9 jit_solution(7973825650771357985)
XLA Ops:
  1.3 286.1 %shard_map.67 = (f32[512,512]{1,0:T(8,128)}, f32[6]{0:T(128)}, f32[1]{0:T(128)}) custom-call(f32[512,512]{1,0:T(8,128)} %h_ref.1, f32[2]{0:T(128)} %bounds_ref.1, s32[1]{0:T(128)S(6)} %copy.10.occ_ref, s32[6]{0:T(128)} %flag_ref.1), custom_call_target="tpu_custom_call" | custom-call | tf_op jit(solution)/shard_map/pallas_call | solution.py:372
  287.4 0.0 copy-start
  287.4 2.3 copy.11
  289.6 0.0 copy-done
  289.6 0.5 copy.12
Async XLA Ops:
  287.4 2.3 copy-start

commit v2 on v0

v2 whole, which is shorter than its diff:
```python
import functools

import jax
import jax.numpy as jnp
from jax import lax
from jax.experimental import pallas as pl
from jax.experimental.pallas import tpu as pltpu
from jax.sharding import PartitionSpec as P

F32 = jnp.float32


def neighbour(dim, row, col):
    if dim == 0:
        return row + 1 - 2 * (row % 2), col
    return row, (col + 2) % 4


def kernel(steps, h_ref, bounds_ref, occ_ref, flag_ref, dens_ref, occs_ref, energy_ref, x_ref, stage, red, z_send, z_recv, y_send,
           y_recv, f_send, f_recv, i_send, i_recv, d_send, d_recv, w_send, w_recv, r_send, r_recv, credit):
    block = h_ref.shape[0]
    half = block // 2
    order = 4 * block
    spin, row, col = lax.axis_index("spin"), lax.axis_index("row"), lax.axis_index("col")
    core = col % 2
    partner = (row, col + 1 - 2 * core)
    odd = (row + col // 2) % 2

    def at(start, size):
        return pl.ds(pl.multiple_of(start, 8), size)

    def lanes(start, size):
        return pl.ds(pl.multiple_of(start, min(128, size)), size)

    def remote(src, dst, send, recv, where):
        return pltpu.make_async_remote_copy(
            src_ref=src, dst_ref=dst, send_sem=send, recv_sem=recv, device_id=(spin,) + tuple(where), device_id_type=pl.DeviceIdType.MESH
        )

    others = [(dr, dc) for dr in range(4) for dc in range(4) if dr or dc]
    barrier = pltpu.get_barrier_semaphore()
    for dr, dc in others:
        pl.semaphore_signal(
            barrier, inc=1, device_id=(spin, (row + dr) % 4, (col + dc) % 4), device_id_type=pl.DeviceIdType.MESH
        )
    pl.semaphore_wait(barrier, len(others))

    def guarded(src, which, run):
        if which == 2:
            pl.when(src[0] == src[1])(run)
        else:
            run()

    def quadrant(src, which):
        low = jnp.where(src[0] > src[1], half, 0)
        return ((0, half), (low, low), (half, half))[which]

    def region(src, which):
        qr, qc = quadrant(src, which)
        return x_ref.at[1, at(src[0] * block + qr, half), lanes(src[1] * block + qc, half)]

    def own_region(which):
        qr, qc = quadrant((row, col), which)
        return h_ref.at[at(qr, half), lanes(qc, half)]

    def each(src, run):
        for which in range(3):
            guarded(src, which, functools.partial(run, which))

    x_ref[1, at(row * block, block), lanes(col * block, block)] = h_ref[...]
    stage[...] = jnp.zeros_like(stage)
    across = (row, (col + 2) % 4)
    rows = (row, row + 1 - 2 * (row % 2), (row + 2) % 4, 3 - row)
    mine = [(r, col) for r in rows]
    theirs = [(r, across[1]) for r in rows]

    def z_out(k, which):
        spot = region(mine[0], which)
        return remote(own_region(which), spot, z_send.at[3 * k + which], z_recv.at[3 * k + which], mine[k])

    def z_in(k, which):
        spot = region(mine[k], which)
        return remote(spot, spot, z_send.at[3 * k + which], z_recv.at[3 * k + which], mine[k])

    def y_out(k, which):
        spot = region(mine[k], which)
        return remote(own_region(which) if k == 0 else spot, spot, y_send.at[3 * k + which], y_recv.at[3 * k + which], across)

    def y_in(k, which):
        spot = region(theirs[k], which)
        return remote(spot, spot, y_send.at[3 * k + which], y_recv.at[3 * k + which], across)

    def f_out(k, which):
        src = (mine + theirs)[k]
        spot = region(src, which)
        return remote(own_region(which) if k == 0 else spot, spot, f_send.at[3 * k + which], f_recv.at[3 * k + which], partner)

    def f_in(k, which):
        src = (mine + theirs)[k]
        spot = region((src[0], src[1] + 1 - 2 * core), which)
        return remote(spot, spot, f_send.at[3 * k + which], f_recv.at[3 * k + which], partner)

    each(mine[0], lambda which: y_out(0, which).start())
    for k in (1, 2, 3):
        each(mine[0], lambda which, k=k: z_out(k, which).start())
    each(mine[0], lambda which: f_out(0, which).start())
    for k in range(4):
        if k:
            def arrived(which, k=k):
                z_in(k, which).wait_recv()
                y_out(k, which).start()
                f_out(k, which).start()

            each(mine[k], arrived)

        def crossed(which, k=k):
            y_in(k, which).wait_recv()
            f_out(4 + k, which).start()

        each(theirs[k], crossed)
    for k in range(8):
        each(((mine + theirs)[k][0], (mine + theirs)[k][1] + 1 - 2 * core), lambda which, k=k: f_in(k, which).wait_recv())
    for k in range(8):
        each((mine + theirs)[k], lambda which, k=k: f_out(k, which).wait_send())
    for k in range(4):
        each(mine[k], lambda which, k=k: y_out(k, which).wait_send())
    for k in (1, 2, 3):
        each(mine[0], lambda which, k=k: z_out(k, which).wait_send())

    quad_eye = lax.broadcasted_iota(jnp.int32, (half, half), 0) == lax.broadcasted_iota(jnp.int32, (half, half), 1)
    trace = jnp.zeros((half, half), F32)
    for k in range(8):
        trace = trace + x_ref[1, k * half:(k + 1) * half, k * half:(k + 1) * half]
    trace = jnp.where(quad_eye, trace, 0.0)
    chem = jnp.sum(jnp.sum(trace, axis=0, keepdims=True), axis=1, keepdims=True) / order
    occupied = jnp.full((1, 1), occ_ref[0], jnp.int32).astype(F32)
    scale = jnp.minimum(occupied / (bounds_ref[1] - chem), (order - occupied) / (chem - bounds_ref[0])) / order
    shift = occupied / order

    def convert(n, carry):
        i, j = n // 4, n % 4
        low = jnp.where(i > j, half, 0)

        def one(qr, qc):
            eye = jnp.logical_and(quad_eye, i * block + qr == j * block + qc)
            value = x_ref[1, at(i * block + qr, half), lanes(j * block + qc, half)]
            value = scale * (jnp.where(eye, chem, 0.0) - value) + jnp.where(eye, shift, 0.0)
            x_ref[0, at(i * block + qr, half), lanes(j * block + qc, half)] = value
            x_ref[0, at(j * block + qc, half), lanes(i * block + qr, half)] = value.T

        one(0, half)
        one(low, low)

        @pl.when(i == j)
        def _():
            one(half, half)

        return carry

    lax.fori_loop(0, 16, convert, 0)

    def sigma(flip, i):
        return i + flip * (3 - 2 * i)

    def between(flip, who):
        return sigma(flip, 0) * block + who * half, sigma(flip, 1) * block

    def product(cur, r0, c0, height, width, flag):
        got = jnp.dot(
            x_ref[cur, at(r0, height), :], x_ref[cur, :, lanes(c0, width)], precision=lax.Precision.HIGHEST, preferred_element_type=F32
        )
        old = x_ref[cur, at(r0, height), lanes(c0, width)]
        return jnp.where(flag == 1, got, 2.0 * old - got)

    near = (neighbour(0, row, col), neighbour(2, row, col))
    sources = near + (partner,)

    def signal_credit():
        for n, where in enumerate(sources):
            pl.semaphore_signal(credit.at[n], inc=1, device_id=(spin,) + where, device_id_type=pl.DeviceIdType.MESH)

    def take_credit():
        for n in range(3):
            pl.semaphore_wait(credit.at[n], 1)

    def lane_sums(value):
        total = value[:, :128]
        for k in range(1, block // 128):
            total = total + value[:, k * 128:(k + 1) * 128]
        return jnp.sum(total, axis=0, keepdims=True)

    def squares(cur):
        own = x_ref[cur, at(row * block, block), lanes(col * block, block)]
        return lane_sums(own * own)

    quarter = half // 2

    def rect(slot, r0, c0, height, width):
        return x_ref.at[slot, at(r0, height), lanes(c0, width)]

    def piece(flip, who, k):
        d0 = sigma(flip, who) * block
        if k == 0:
            return d0, d0, block
        if k == 1:
            return d0 + half, d0 + half, half
        return between(flip, who) + (block,)

    def part_copy(flip, who, k, part, slot, send, recv, where):
        r0, c0, width = piece(flip, who, k)
        spot = rect(slot, r0 + part * quarter, c0, quarter, width)
        n = slot * 6 + k * 2 + part
        return remote(spot, spot, send.at[n], recv.at[n], where)

    def outward(k, part, slot):
        return part_copy(odd, core, k, part, slot, i_send, i_recv, near[part])

    def inward(k, part, slot):
        return part_copy(1 - odd, core, k, part, slot, i_send, i_recv, near[part])

    def passed(who, k, part, slot):
        return part_copy(1 - odd, who, k, part, slot, w_send, w_recv, partner)

    def direct(who, k, slot):
        if k < 3:
            r0, c0, width = piece(odd, who, k)
            if k == 0:
                spots = [rect(slot, r0, c0, half, block), rect(slot, c0 + half, r0, half, half)]
            elif k == 1:
                spots = [rect(slot, r0, c0, half, half)]
            else:
                spots = [rect(slot, r0, c0, half, block), rect(slot, c0, r0, block, half)]
        else:
            r0, c0 = sigma(odd, who) * block, sigma(odd, k - 1) * block
            spots = [rect(slot, r0, c0, block, block), rect(slot, c0, r0, block, block)]
        return [remote(spot, spot, d_send.at[slot * 10 + 2 * k + n], d_recv.at[slot * 10 + 2 * k + n], partner) for n, spot in enumerate(spots)]

    def send_piece(k, slot):
        for part in range(2):
            outward(k, part, slot).start()
        for copy in direct(core, k, slot):
            copy.start()

    def relay(k, slot):
        for part in range(2):
            inward(k, part, slot).wait_recv()
            passed(core, k, part, slot).start()

    def partner_settled(slot):
        for k in (0, 1, 3, 4):
            for copy in direct(1 - core, k, slot):
                copy.wait_recv()

    def remote_settled(slot):
        for k in range(3):
            for part in range(2):
                passed(1 - core, k, part, slot).wait_recv()
        for who in range(2):
            r0, c0, _ = piece(1 - odd, who, 0)
            x_ref[slot, at(c0 + half, half), lanes(r0, half)] = x_ref[slot, at(r0, half), lanes(c0 + half, half)].T
            r0, c0, _ = piece(1 - odd, who, 2)
            x_ref[slot, at(c0, block), lanes(r0, half)] = x_ref[slot, at(r0, half), lanes(c0, block)].T

    def drained(slot):
        for k in range(5):
            for copy in direct(core, k, slot):
                copy.wait_send()
        for k in range(3):
            for part in range(2):
                outward(k, part, slot).wait_send()
                passed(core, k, part, slot).wait_send()

    def step(t, carry):
        cur, nxt = t % 2, 1 - t % 2
        flag = flag_ref[t]

        r0, c0, _ = piece(odd, core, 0)
        new = product(cur, r0, c0, half, block, flag)
        take_credit()
        x_ref[nxt, at(r0, half), lanes(c0, block)] = new
        x_ref[nxt, at(c0 + half, half), lanes(r0, half)] = new[:, half:].T
        send_piece(0, nxt)

        r0, c0, _ = piece(odd, core, 1)
        x_ref[nxt, at(r0, half), lanes(c0, half)] = product(cur, r0, c0, half, half, flag)
        send_piece(1, nxt)

        @pl.when(t > 0)
        def _():
            partner_settled(cur)

        r0, c0, _ = piece(odd, core, 2)
        new = product(cur, r0, c0, half, block, flag)
        x_ref[nxt, at(r0, half), lanes(c0, block)] = new
        x_ref[nxt, at(c0, block), lanes(r0, half)] = new.T
        send_piece(2, nxt)

        @pl.when(t > 0)
        def _():
            remote_settled(cur)

        stage[pl.ds(t, 1), :] = squares(cur)

        def wide(k, carry):
            r0, c0 = sigma(odd, core) * block, sigma(odd, 2 + k) * block
            new = product(cur, r0, c0, block, block, flag)
            x_ref[nxt, at(r0, block), lanes(c0, block)] = new
            x_ref[nxt, at(c0, block), lanes(r0, block)] = new.T

            @pl.when(k == 0)
            def _():
                for copy in direct(core, 3, nxt):
                    copy.start()
                relay(0, nxt)
                relay(1, nxt)

            return carry

        lax.fori_loop(0, 2, wide, 0)
        for copy in direct(core, 4, nxt):
            copy.start()
        relay(2, nxt)
        for copy in direct(1 - core, 2, nxt):
            copy.wait_recv()

        @pl.when(t > 0)
        def _():
            drained(cur)

        @pl.when(t < steps - 2)
        def _():
            signal_credit()

        return carry

    signal_credit()
    lax.fori_loop(0, steps - 1, step, 0)
    last = (steps - 1) % 2
    partner_settled(last)
    remote_settled(last)

    stage[steps - 1:steps, :] = squares(last)
    final = product(last, row * block, col * block, block, block, flag_ref[steps - 1])
    dens_ref[...] = final
    drained(last)
    stage[steps:steps + 1, :] = lane_sums(final * h_ref[...])

    red[row * 4 + col] = stage[...]
    for n, (dr, dc) in enumerate(others):
        remote(stage, red.at[row * 4 + col], r_send.at[n], r_recv.at[n], ((row + dr) % 4, (col + dc) % 4)).start()
    for n, (dr, dc) in enumerate(others):
        spot = red.at[((row - dr) % 4) * 4 + (col - dc) % 4]
        remote(stage, spot, r_send.at[n], r_recv.at[n], partner).wait_recv()
    total = red[0]
    for n in range(1, 16):
        total = total + red[n]
    for n in range(steps):
        occs_ref[n] = jnp.sum(total[n:n + 1, :])
    energy_ref[0] = 2.0 * jnp.sum(total[steps:steps + 1, :])
    for n, (dr, dc) in enumerate(others):
        remote(stage, red.at[row * 4 + col], r_send.at[n], r_recv.at[n], ((row + dr) % 4, (col + dc) % 4)).wait_send()


def solution(mesh):
    def local_run(ham_block, bounds, occ_count, branches):
        block, steps = ham_block.shape[0], branches.shape[0]
        order = 4 * block
        dma = pltpu.SemaphoreType.DMA
        vmem = pl.BlockSpec(memory_space=pltpu.VMEM)
        smem = pl.BlockSpec(memory_space=pltpu.SMEM)
        return pl.pallas_call(
            functools.partial(kernel, steps),
            out_shape=(
                jax.ShapeDtypeStruct((block, block), F32),
                jax.ShapeDtypeStruct((steps,), F32),
                jax.ShapeDtypeStruct((1,), F32),
            ),
            in_specs=[vmem, smem, smem, smem],
            out_specs=(vmem, smem, smem),
            scratch_shapes=[
                pltpu.VMEM((2, order, order), F32),
                pltpu.VMEM((8, 128), F32),
                pltpu.VMEM((16, 8, 128), F32),
                dma((12,)), dma((12,)), dma((12,)), dma((12,)), dma((24,)), dma((24,)),
                dma((12,)), dma((12,)), dma((20,)), dma((20,)), dma((12,)), dma((12,)),
                dma((15,)), dma((15,)),
                pltpu.SemaphoreType.REGULAR((3,)),
            ],
            compiler_params=pltpu.CompilerParams(collective_id=0, has_side_effects=True, vmem_limit_bytes=60 * 1024 * 1024),
        )(ham_block, bounds, occ_count, branches)

    return jax.shard_map(
        local_run,
        mesh=mesh,
        in_specs=(P(("spin", "row"), "col"), P("spin"), P("spin"), P("spin")),
        out_specs=(P(("spin", "row"), "col"), P("spin"), P("spin")),
        check_vma=False,
    )
```

time: 800 us -> 246 us (0.31)
  starting transfers between devices: 461 us -> 0 us
  Pallas kernels: 0 us -> 240 us
  waiting for transfers between devices: 176 us -> 0 us
  blocking collectives: 87.2 us -> 0 us
  matrix products: 50.5 us -> 0 us
    ppermute x48 -> x0, starting transfers between devices: 461 us -> none  [the longest x18 286 us: grid_square(): left_block = lax.ppermute(left_block, 'col', shift_perm)]
    pallas_call x0 -> x1, Pallas kernels: none -> 240 us  [local_run(): pl.pallas_call(functools.partial(kernel, steps), out_shape=(jax.ShapeDtyp...]
    ppermute x48 -> x0, waiting for transfers between devices: 176 us -> none  [the longest x18 139 us: grid_square(): right_block = lax.ppermute(right_block, 'row', shift_perm)]
    psum x2 -> x0, blocking collectives: 87.2 us -> none  [the longest x1 51.7 us: local_run(): occ_list.append(lax.psum(jnp.sum(density * density), ('row', 'col')))]
    dot_general x24 -> x0, matrix products: 50.5 us -> none  [block_product(): jnp.dot(left_block, right_block, preferred_element_type=jnp.float32, prec...]
  transfers between devices with their start and end apart: 48 -> 0, of which waited for: 24 -> 0; matrix products, arithmetic and copies ran while one was open for 4% -> 0% of each run, Pallas kernels for 0% -> 0%
where the time goes in v2:
time: 246 us
  Pallas kernels  240 us (98%)
  between operations  3.05 us (1%)
  local copies, waits for them, and re-layouts  2.78 us (1%)
    pallas_call x1, Pallas kernels, local_run(): pl.pallas_call(functools.partial(kernel, steps), out_shape=(jax.ShapeDtyp...  240 us

profile of v2, /device:TPU:0, one launch (start us, length us, event | category | flops | bytes accessed | tf_op | source)
XLA Modules:
  0.0 246.0 jit_solution(6093684872394182962)
XLA Ops:
  1.3 240.2 %shard_map.67 = (f32[512,512]{1,0:T(8,128)}, f32[6]{0:T(128)}, f32[1]{0:T(128)}) custom-call(f32[512,512]{1,0:T(8,128)} %h_ref.1, f32[2]{0:T(128)} %bounds_ref.1, s32[1]{0:T(128)S(6)} %copy.10.occ_ref, s32[6]{0:T(128)} %flag_ref.1), custom_call_target="tpu_custom_call" | custom-call | tf_op jit(solution)/shard_map/pallas_call | solution.py:371
  241.4 0.0 copy-start
  241.5 2.3 copy.11
  243.7 0.0 copy-done
  243.7 0.5 copy.12
Async XLA Ops:
  241.4 2.3 copy-start

commit v3 on v2

v3 whole, which is shorter than its diff:
```python
import functools

import jax
import jax.numpy as jnp
from jax import lax
from jax.experimental import pallas as pl
from jax.experimental.pallas import tpu as pltpu
from jax.sharding import PartitionSpec as P

F32 = jnp.float32


def neighbour(dim, row, col):
    if dim == 0:
        return row + 1 - 2 * (row % 2), col
    return row, (col + 2) % 4


def kernel(steps, h_ref, bounds_ref, occ_ref, flag_ref, dens_ref, occs_ref, energy_ref, x_ref, stage, red, z_send, z_recv, e_send,
           e_recv, y_send, y_recv, f_send, f_recv, i_send, i_recv, d_send, d_recv, w_send, w_recv, r_send, r_recv, credit):
    block = h_ref.shape[0]
    half = block // 2
    order = 4 * block
    spin, row, col = lax.axis_index("spin"), lax.axis_index("row"), lax.axis_index("col")
    core = col % 2
    partner = (row, col + 1 - 2 * core)
    odd = (row + col // 2) % 2

    def at(start, size):
        return pl.ds(pl.multiple_of(start, 8), size)

    def lanes(start, size):
        return pl.ds(pl.multiple_of(start, min(128, size)), size)

    def remote(src, dst, send, recv, where):
        return pltpu.make_async_remote_copy(
            src_ref=src, dst_ref=dst, send_sem=send, recv_sem=recv, device_id=(spin,) + tuple(where), device_id_type=pl.DeviceIdType.MESH
        )

    others = [(dr, dc) for dr in range(4) for dc in range(4) if dr or dc]
    barrier = pltpu.get_barrier_semaphore()
    for dr, dc in others:
        pl.semaphore_signal(
            barrier, inc=1, device_id=(spin, (row + dr) % 4, (col + dc) % 4), device_id_type=pl.DeviceIdType.MESH
        )
    pl.semaphore_wait(barrier, len(others))

    def quadrant(src, which):
        low = jnp.where(src[0] > src[1], half, 0)
        return ((0, half), (low, low), (half, half))[which]

    def region(src, which):
        qr, qc = quadrant(src, which)
        return x_ref.at[1, at(src[0] * block + qr, half), lanes(src[1] * block + qc, half)]

    def own_region(which):
        qr, qc = quadrant((row, col), which)
        return h_ref.at[at(qr, half), lanes(qc, half)]

    def each(src, run, *conditions):
        for which in range(3):
            terms = list(conditions) + ([src[0] == src[1]] if which == 2 else [])
            if terms:
                pl.when(functools.reduce(jnp.logical_and, terms))(functools.partial(run, which))
            else:
                run(which)

    x_ref[1, at(row * block, block), lanes(col * block, block)] = h_ref[...]
    stage[...] = jnp.zeros_like(stage)
    far = (col + 2) % 4
    end = 3 * core

    def span(src, which, send, recv, n, where, own=False):
        spot = region(src, which)
        return remote(own_region(which) if own else spot, spot, send.at[3 * n + which], recv.at[3 * n + which], where)

    def z_out(turn, way, which):
        sign = 1 - 2 * way
        return span((row + sign * turn, col), which, z_send, z_recv, 2 * turn + way, (row - sign, col), turn == 0)

    def z_in(turn, way, which):
        sign = 1 - 2 * way
        return span((row + sign * turn, col), which, z_send, z_recv, 2 * (turn - 1) + way, (row + sign, col))

    def y_out(r, which, own=False):
        return span((r, col), which, y_send, y_recv, r, (row, far), own)

    def y_in(r, which):
        return span((r, far), which, y_send, y_recv, r, (row, far))

    def e_out(which):
        return span((end, far), which, e_send, e_recv, 0, (row + 1 - 2 * core, col))

    def e_in(which):
        return span((end, far), which, e_send, e_recv, 0, (row - 1 + 2 * core, col))

    def f_out(c, r, which, own=False):
        return span((r, c), which, f_send, f_recv, 4 * (c // 2) + r, partner, own)

    def f_in(c, r, which):
        return span((r, c + 1 - 2 * core), which, f_send, f_recv, 4 * (c // 2) + r, partner)

    def has(r):
        return jnp.logical_and(r >= 0, r <= 3)

    def crosses(r):
        return jnp.logical_or(r != end, row == end)

    def first(which):
        y_out(row, which, True).start()

        @pl.when(row > 0)
        def _():
            z_out(0, 0, which).start()

        @pl.when(row < 3)
        def _():
            z_out(0, 1, which).start()

        f_out(col, row, which, True).start()

    each((row, col), first)

    def take_line(turn):
        for way in range(2):
            sign = 1 - 2 * way
            r = row + sign * turn

            def arrived(which):
                z_in(turn, way, which).wait_recv()
                if turn < 3:
                    @pl.when(has(row - sign))
                    def _():
                        z_out(turn, way, which).start()

                @pl.when(crosses(r))
                def _():
                    y_out(r, which).start()

                f_out(col, r, which).start()

            each((r, col), arrived, has(r))

    def take_across(r):
        def arrived(which):
            y_in(r, which).wait_recv()
            f_out(far, r, which).start()

        each((r, far), arrived, has(r), crosses(r))

    def hand_on(which):
        @pl.when(has(row + 1 - 2 * core))
        def _():
            e_out(which).start()

    take_line(1)
    take_across(row)
    each((end, far), hand_on, row == end)
    take_line(2)
    take_across(row - 1)
    take_across(row + 1)
    take_line(3)

    def ended(which):
        e_in(which).wait_recv()
        hand_on(which)
        f_out(far, end, which).start()

    each((end, far), ended, row != end)
    for apart in (2, 3):
        take_across(row - apart)
        take_across(row + apart)
    for c in (col, far):
        for r in range(4):
            each((r, c + 1 - 2 * core), lambda which, c=c, r=r: f_in(c, r, which).wait_recv())

    def gather_drained():
        for c in (col, far):
            for r in range(4):
                each((r, c), lambda which, c=c, r=r: f_out(c, r, which).wait_send())
        for r in range(4):
            each((r, col), lambda which, r=r: y_out(r, which).wait_send(), crosses(r))
        for turn in range(3):
            for way in range(2):
                sign = 1 - 2 * way
                r = row + sign * turn
                each((r, col), lambda which, turn=turn, way=way: z_out(turn, way, which).wait_send(), has(r), has(row - sign))
        each((end, far), lambda which: e_out(which).wait_send(), has(row + 1 - 2 * core))

    gather_drained()

    quad_eye = lax.broadcasted_iota(jnp.int32, (half, half), 0) == lax.broadcasted_iota(jnp.int32, (half, half), 1)
    trace = jnp.zeros((half, half), F32)
    for k in range(8):
        trace = trace + x_ref[1, k * half:(k + 1) * half, k * half:(k + 1) * half]
    trace = jnp.where(quad_eye, trace, 0.0)
    chem = jnp.sum(jnp.sum(trace, axis=0, keepdims=True), axis=1, keepdims=True) / order
    occupied = jnp.full((1, 1), occ_ref[0], jnp.int32).astype(F32)
    scale = jnp.minimum(occupied / (bounds_ref[1] - chem), (order - occupied) / (chem - bounds_ref[0])) / order
    shift = occupied / order

    def convert(n, carry):
        i, j = n // 4, n % 4
        low = jnp.where(i > j, half, 0)

        def one(qr, qc):
            eye = jnp.logical_and(quad_eye, i * block + qr == j * block + qc)
            value = x_ref[1, at(i * block + qr, half), lanes(j * block + qc, half)]
            value = scale * (jnp.where(eye, chem, 0.0) - value) + jnp.where(eye, shift, 0.0)
            x_ref[0, at(i * block + qr, half), lanes(j * block + qc, half)] = value
            x_ref[0, at(j * block + qc, half), lanes(i * block + qr, half)] = value.T

        one(0, half)
        one(low, low)

        @pl.when(i == j)
        def _():
            one(half, half)

        return carry

    lax.fori_loop(0, 16, convert, 0)

    def sigma(flip, i):
        return i + flip * (3 - 2 * i)

    def between(flip, who):
        return sigma(flip, 0) * block + who * half, sigma(flip, 1) * block

    def single(flip, who):
        return who * block + half, (2 + who + flip * (1 - 2 * who)) * block

    def common(flip, who, k):
        return (who + flip * (k - who)) * block, (2 + k + flip * (1 - who - k)) * block

    def product(cur, r0, c0, height, width, flag):
        got = jnp.dot(
            x_ref[cur, at(r0, height), :], x_ref[cur, :, lanes(c0, width)], precision=lax.Precision.HIGHEST, preferred_element_type=F32
        )
        old = x_ref[cur, at(r0, height), lanes(c0, width)]
        return jnp.where(flag == 1, got, 2.0 * old - got)

    near = (neighbour(0, row, col), neighbour(2, row, col))
    sources = near + (partner,)

    def signal_credit():
        for n, where in enumerate(sources):
            pl.semaphore_signal(credit.at[n], inc=1, device_id=(spin,) + where, device_id_type=pl.DeviceIdType.MESH)

    def take_credit():
        for n in range(3):
            pl.semaphore_wait(credit.at[n], 1)

    def lane_sums(value):
        total = value[:, :128]
        for k in range(1, block // 128):
            total = total + value[:, k * 128:(k + 1) * 128]
        return jnp.sum(total, axis=0, keepdims=True)

    def squares(cur):
        own = x_ref[cur, at(row * block, block), lanes(col * block, block)]
        return lane_sums(own * own)

    quarter = half // 2

    def rect(slot, r0, c0, height, width):
        return x_ref.at[slot, at(r0, height), lanes(c0, width)]

    def piece(flip, who, k):
        d0 = sigma(flip, who) * block
        if k == 0:
            return d0, d0, block
        if k == 1:
            return d0 + half, d0 + half, half
        return (between if k == 2 else single)(flip, who) + (block,)

    def part_copy(flip, who, k, part, slot, send, recv, where):
        r0, c0, width = piece(flip, who, k)
        spot = rect(slot, r0 + part * quarter, c0, quarter, width)
        n = slot * 8 + k * 2 + part
        return remote(spot, spot, send.at[n], recv.at[n], where)

    def sender(who, k):
        return who + odd * (1 - 2 * who) if k == 3 else who

    def outward(k, part, slot):
        to_row, to_col = near[part]
        if k == 3:
            to_col = to_col + (1 - odd) * (1 - 2 * core)
        return part_copy(odd, core, k, part, slot, i_send, i_recv, (to_row, to_col))

    def inward(k, part, slot):
        return part_copy(1 - odd, sender(core, k), k, part, slot, i_send, i_recv, near[part])

    def passed(who, k, part, slot):
        return part_copy(1 - odd, sender(who, k), k, part, slot, w_send, w_recv, partner)

    def direct(who, k, slot):
        if k < 4:
            r0, c0, width = piece(odd, who, k)
        else:
            r0, c0 = common(odd, who, k - 4)
        if k == 0:
            spots = [rect(slot, r0, c0, half, block), rect(slot, c0 + half, r0, half, half)]
        elif k == 1:
            spots = [rect(slot, r0, c0, half, half)]
        else:
            spots = [rect(slot, r0, c0, half, block), rect(slot, c0, r0, block, half)]
        return [remote(spot, spot, d_send.at[slot * 12 + 2 * k + n], d_recv.at[slot * 12 + 2 * k + n], partner) for n, spot in enumerate(spots)]

    def send_piece(k, slot):
        if k < 4:
            for part in range(2):
                outward(k, part, slot).start()
        for copy in direct(core, k, slot):
            copy.start()

    def relay(k, slot):
        for part in range(2):
            inward(k, part, slot).wait_recv()
            passed(core, k, part, slot).start()

    def mirror(flip, who, k, slot):
        r0, c0, _ = piece(flip, who, k)
        if k == 0:
            x_ref[slot, at(c0 + half, half), lanes(r0, half)] = x_ref[slot, at(r0, half), lanes(c0 + half, half)].T
        else:
            x_ref[slot, at(c0, block), lanes(r0, half)] = x_ref[slot, at(r0, half), lanes(c0, block)].T

    def early(slot):
        relay(3, slot)
        for copy in direct(1 - core, 2, slot):
            copy.wait_recv()
        mirror(1 - odd, sender(core, 3), 3, slot)

    def settled(slot):
        relay(2, slot)
        for k in (0, 1, 3, 4, 5):
            for copy in direct(1 - core, k, slot):
                copy.wait_recv()
        for k in (0, 1, 3, 2):
            for part in range(2):
                passed(1 - core, k, part, slot).wait_recv()
        mirror(1 - odd, sender(1 - core, 3), 3, slot)
        for who in range(2):
            mirror(1 - odd, who, 0, slot)
            mirror(1 - odd, who, 2, slot)

    def drained(slot):
        for k in range(6):
            for copy in direct(core, k, slot):
                copy.wait_send()
        for k in range(4):
            for part in range(2):
                outward(k, part, slot).wait_send()
                passed(core, k, part, slot).wait_send()

    def work(u, carry):
        t, m = u // 5, u % 5
        cur, nxt = t % 2, 1 - t % 2
        flag = flag_ref[t]
        live = t < steps - 1

        def on(where, *conditions):
            for condition in conditions:
                where = jnp.logical_and(where, condition)
            return pl.when(where)

        @on(m == 0, t > 0)
        def _():
            early(cur)

        @on(m == 0, t == steps - 1)
        def _():
            settled(cur)
            stage[pl.ds(t, 1), :] = squares(cur)

        @on(m == 1, live)
        def _():
            r0, c0, _ = piece(odd, core, 1)
            x_ref[nxt, at(r0, half), lanes(c0, half)] = product(cur, r0, c0, half, half, flag)
            send_piece(1, nxt)

            @pl.when(t > 0)
            def _():
                settled(cur)

            stage[pl.ds(t, 1), :] = squares(cur)

        @on(m == 4)
        def _():
            relay(0, nxt)
            relay(1, nxt)

        d0 = piece(odd, core, 0)[:2]
        spots = (d0, single(odd, core), between(odd, core), common(odd, core, 0), common(odd, core, 1))
        r0, c0 = row * block + m * half, col * block
        for k, (r1, c1) in enumerate(spots):
            r0 = jnp.where(jnp.logical_and(live, m == k), r1, r0)
            c0 = jnp.where(jnp.logical_and(live, m == k), c1, c0)
        new = product(cur, r0, c0, half, block, flag)

        @on(m == 0, live)
        def _():
            take_credit()

        x_ref[nxt, at(r0, half), lanes(c0, block)] = new

        @pl.when(live)
        def _():
            x_ref[nxt, at(c0, block), lanes(r0, half)] = new.T

        for n, k in enumerate((0, 3, 2, 4, 5)):
            @on(m == n, live)
            def _():
                send_piece(k, nxt)

        @on(m == 4, t > 0)
        def _():
            drained(cur)

        @on(m == 4, t < steps - 2)
        def _():
            signal_credit()

        return carry

    signal_credit()
    lax.fori_loop(0, 5 * (steps - 1) + 2, work, 0)
    last = (steps - 1) % 2

    final = x_ref[1 - last, at(row * block, block), lanes(col * block, block)]
    dens_ref[...] = final
    stage[steps:steps + 1, :] = lane_sums(final * h_ref[...])
    drained(last)

    red[row * 4 + col] = stage[...]
    for n, (dr, dc) in enumerate(others):
        remote(stage, red.at[row * 4 + col], r_send.at[n], r_recv.at[n], ((row + dr) % 4, (col + dc) % 4)).start()
    for n, (dr, dc) in enumerate(others):
        spot = red.at[((row - dr) % 4) * 4 + (col - dc) % 4]
        remote(stage, spot, r_send.at[n], r_recv.at[n], partner).wait_recv()
    total = red[0]
    for n in range(1, 16):
        total = total + red[n]
    for n in range(steps):
        occs_ref[n] = jnp.sum(total[n:n + 1, :])
    energy_ref[0] = 2.0 * jnp.sum(total[steps:steps + 1, :])
    for n, (dr, dc) in enumerate(others):
        remote(stage, red.at[row * 4 + col], r_send.at[n], r_recv.at[n], ((row + dr) % 4, (col + dc) % 4)).wait_send()


def solution(mesh):
    def local_run(ham_block, bounds, occ_count, branches):
        block, steps = ham_block.shape[0], branches.shape[0]
        order = 4 * block
        dma = pltpu.SemaphoreType.DMA
        vmem = pl.BlockSpec(memory_space=pltpu.VMEM)
        smem = pl.BlockSpec(memory_space=pltpu.SMEM)
        return pl.pallas_call(
            functools.partial(kernel, steps),
            out_shape=(
                jax.ShapeDtypeStruct((block, block), F32),
                jax.ShapeDtypeStruct((steps,), F32),
                jax.ShapeDtypeStruct((1,), F32),
            ),
            in_specs=[vmem, smem, smem, smem],
            out_specs=(vmem, smem, smem),
            scratch_shapes=[
                pltpu.VMEM((2, order, order), F32),
                pltpu.VMEM((8, 128), F32),
                pltpu.VMEM((16, 8, 128), F32),
                dma((18,)), dma((18,)), dma((3,)), dma((3,)), dma((12,)), dma((12,)), dma((24,)), dma((24,)),
                dma((16,)), dma((16,)), dma((24,)), dma((24,)), dma((16,)), dma((16,)),
                dma((15,)), dma((15,)),
                pltpu.SemaphoreType.REGULAR((3,)),
            ],
            compiler_params=pltpu.CompilerParams(collective_id=0, has_side_effects=True, vmem_limit_bytes=60 * 1024 * 1024),
        )(ham_block, bounds, occ_count, branches)

    return jax.shard_map(
        local_run,
        mesh=mesh,
        in_specs=(P(("spin", "row"), "col"), P("spin"), P("spin"), P("spin")),
        out_specs=(P(("spin", "row"), "col"), P("spin"), P("spin")),
        check_vma=False,
    )
```

time: 246 us -> 211 us (0.86)
  Pallas kernels: 240 us -> 205 us
    pallas_call x1, Pallas kernels: 240 us -> 205 us  [local_run(): pl.pallas_call(functools.partial(kernel, steps), out_shape=(jax.ShapeDtyp...]
where the time goes in v3:
time: 211 us
  Pallas kernels  205 us (97%)
  between operations  3.05 us (1%)
  local copies, waits for them, and re-layouts  2.78 us (1%)
    pallas_call x1, Pallas kernels, local_run(): pl.pallas_call(functools.partial(kernel, steps), out_shape=(jax.ShapeDtyp...  205 us

profile of v3, /device:TPU:0, one launch (start us, length us, event | category | flops | bytes accessed | tf_op | source)
XLA Modules:
  0.0 210.8 jit_solution(15879080810288909100)
XLA Ops:
  1.3 205.0 %shard_map.67 = (f32[512,512]{1,0:T(8,128)}, f32[6]{0:T(128)}, f32[1]{0:T(128)}) custom-call(f32[512,512]{1,0:T(8,128)} %h_ref.1, f32[2]{0:T(128)} %bounds_ref.1, s32[1]{0:T(128)S(6)} %copy.10.occ_ref, s32[6]{0:T(128)} %flag_ref.1), custom_call_target="tpu_custom_call" | custom-call | tf_op jit(solution)/shard_map/pallas_call | solution.py:460
  206.3 0.0 copy-start
  206.3 2.3 %copy.11 = f32[512,512]{1,0:T(8,128)} copy(f32[512,512]{1,0:T(8,128)} %get-tuple-element.6) | data formatting | bytes 2097152
  208.5 0.0 copy-done
  208.5 0.5 copy.12
Async XLA Ops:
  206.3 2.3 %copy-start = (f32[6]{0:T(128)S(1)}, f32[6]{0:T(128)}, u32[]{:S(2)}) copy-start(f32[6]{0:T(128)} %get-tuple-element.7) | copy-start | bytes 76

commit v4 on v3

--- a/solution.py
+++ b/solution.py
@@ -16,8 +16,8 @@
     return row, (col + 2) % 4
 
 
-def kernel(steps, h_ref, bounds_ref, occ_ref, flag_ref, dens_ref, occs_ref, energy_ref, x_ref, stage, red, z_send, z_recv, e_send,
-           e_recv, y_send, y_recv, f_send, f_recv, i_send, i_recv, d_send, d_recv, w_send, w_recv, r_send, r_recv, credit):
+def kernel(steps, h_ref, bounds_ref, occ_ref, flag_ref, dens_ref, occs_ref, energy_ref, x_ref, stage, red, traces, t_send, t_recv, z_send, z_recv, e_send,
+           e_recv, y_send, y_recv, f_send, f_recv, s_send, i_recv, h_recv, s_recv, r_send, r_recv, credit):
     block = h_ref.shape[0]
     half = block // 2
     order = 4 * block
@@ -45,6 +45,14 @@
         )
     pl.semaphore_wait(barrier, len(others))
 
+    def await_send(sem, units):
+        spot = x_ref.at[0, pl.ds(0, units * (half * half) // order), :]
+        remote(spot, spot, sem, h_recv.at[0], partner).wait_send()
+
+    def await_recv(sem, units):
+        spot = x_ref.at[0, pl.ds(0, units * (half * half) // order), :]
+        remote(spot, spot, s_send.at[0], sem, partner).wait_recv()
+
     def quadrant(src, which):
         low = jnp.where(src[0] > src[1], half, 0)
         return ((0, half), (low, low), (half, half))[which]
@@ -66,13 +74,17 @@
                 run(which)
 
     x_ref[1, at(row * block, block), lanes(col * block, block)] = h_ref[...]
-    stage[...] = jnp.zeros_like(stage)
     far = (col + 2) % 4
     end = 3 * core
 
-    def span(src, which, send, recv, n, where, own=False):
+    def span(src, which, send, recv, n, where, own=False, merged=False):
         spot = region(src, which)
-        return remote(own_region(which) if own else spot, spot, send.at[3 * n + which], recv.at[3 * n + which], where)
+        recv_sem = recv.at[n] if merged else recv.at[3 * n + which]
+        return remote(own_region(which) if own else spot, spot, send.at[0 if merged else n], recv_sem, where)
+
+    def whole(src, wait):
+        pl.when(src[0] == src[1])(lambda: wait(3))
+        pl.when(src[0] != src[1])(lambda: wait(2))
 
     def z_out(turn, way, which):
         sign = 1 - 2 * way
@@ -95,10 +107,7 @@
         return span((end, far), which, e_send, e_recv, 0, (row - 1 + 2 * core, col))
 
     def f_out(c, r, which, own=False):
-        return span((r, c), which, f_send, f_recv, 4 * (c // 2) + r, partner, own)
-
-    def f_in(c, r, which):
-        return span((r, c + 1 - 2 * core), which, f_send, f_recv, 4 * (c // 2) + r, partner)
+        return span((r, c), which, f_send, f_recv, 4 * (c // 2) + r, partner, own, True)
 
     def has(r):
         return jnp.logical_and(r >= 0, r <= 3)
@@ -119,7 +128,61 @@
 
         f_out(col, row, which, True).start()
 
+    quad_eye = lax.broadcasted_iota(jnp.int32, (half, half), 0) == lax.broadcasted_iota(jnp.int32, (half, half), 1)
+
+    @pl.when(row == col)
+    def _():
+        diagonal = jnp.where(quad_eye, h_ref[:half, :half] + h_ref[half:, half:], 0.0)
+        stage[...] = jnp.zeros_like(stage)
+        for k in range(max(half // 128, 1)):
+            stage[0:1, :min(half, 128)] += jnp.sum(diagonal[:, k * 128:(k + 1) * 128], axis=0, keepdims=True)
+        traces[row] = stage[...]
+        for n, (dr, dc) in enumerate(others):
+            remote(stage, traces.at[row], t_send.at[0], t_recv.at[row], ((row + dr) % 4, (col + dc) % 4)).start()
+
     each((row, col), first)
+
+    for k in range(4):
+        @pl.when(jnp.logical_or(row != k, col != k))
+        def _():
+            remote(stage, traces.at[k], t_send.at[0], t_recv.at[k], partner).wait_recv()
+
+    chem = jnp.sum(jnp.sum(traces[0] + traces[1] + traces[2] + traces[3], axis=0, keepdims=True), axis=1, keepdims=True) / order
+    occupied = jnp.full((1, 1), occ_ref[0], jnp.int32).astype(F32)
+    scale = jnp.minimum(occupied / (bounds_ref[1] - chem), (order - occupied) / (chem - bounds_ref[0])) / order
+    shift = occupied / order
+
+    def convert(r, c, *conditions):
+        def body(which, carry):
+            low = jnp.where(r > c, half, 0)
+            qr = jnp.where(which == 0, 0, jnp.where(which == 1, low, half))
+            qc = jnp.where(which == 0, half, qr)
+            eye = jnp.logical_and(quad_eye, r * block + qr == c * block + qc)
+            value = x_ref[1, at(r * block + qr, half), lanes(c * block + qc, half)]
+            value = scale * (jnp.where(eye, chem, 0.0) - value) + jnp.where(eye, shift, 0.0)
+            x_ref[0, at(r * block + qr, half), lanes(c * block + qc, half)] = value
+            x_ref[0, at(c * block + qc, half), lanes(r * block + qr, half)] = value.T
+            return carry
+
+        def run():
+            lax.fori_loop(0, 2 + jnp.where(r == c, 1, 0), body, 0)
+
+        if conditions:
+            pl.when(functools.reduce(jnp.logical_and, conditions))(run)
+        else:
+            run()
+
+    def from_partner(c, r, *conditions):
+        src = (r, c + 1 - 2 * core)
+
+        def run():
+            whole(src, lambda units: await_recv(f_recv.at[4 * (c // 2) + r], units))
+            convert(*src)
+
+        if conditions:
+            pl.when(functools.reduce(jnp.logical_and, conditions))(run)
+        else:
+            run()
 
     def take_line(turn):
         for way in range(2):
@@ -153,12 +216,22 @@
         def _():
             e_out(which).start()
 
+    convert(row, col)
     take_line(1)
     take_across(row)
     each((end, far), hand_on, row == end)
+    from_partner(col, row)
+    convert(row, far)
+    for r in (row - 1, row + 1):
+        convert(r, col, has(r))
     take_line(2)
-    take_across(row - 1)
-    take_across(row + 1)
+    from_partner(far, row)
+    for r in (row - 1, row + 1):
+        take_across(r)
+        from_partner(col, r, has(r))
+        convert(r, far, has(r), crosses(r))
+    for r in (row - 2, row + 2):
+        convert(r, col, has(r))
     take_line(3)
 
     def ended(which):
@@ -167,59 +240,43 @@
         f_out(far, end, which).start()
 
     each((end, far), ended, row != end)
-    for apart in (2, 3):
-        take_across(row - apart)
-        take_across(row + apart)
-    for c in (col, far):
+    for r in (row - 1, row + 1):
+        from_partner(far, r, has(r), r != 3 - end)
+    for r in (row - 2, row + 2):
+        from_partner(col, r, has(r))
+    for r in (row - 2, row + 2):
+        take_across(r)
+        convert(r, far, has(r), crosses(r))
+    convert(end, far, row != end)
+    for r in (row - 3, row + 3):
+        take_across(r)
+        convert(r, col, has(r))
+        from_partner(col, r, has(r))
+    for r in (row - 2, row + 2):
+        from_partner(far, r, has(r), r != 3 - end)
+    from_partner(far, 3 - end, row != 3 - end)
+    for r in (row - 3, row + 3):
+        convert(r, far, has(r), crosses(r))
+        from_partner(far, r, has(r), r != 3 - end)
+
+    def gather_drained():
+        await_send(f_send.at[0], 18)
         for r in range(4):
-            each((r, c + 1 - 2 * core), lambda which, c=c, r=r: f_in(c, r, which).wait_recv())
-
-    def gather_drained():
-        for c in (col, far):
-            for r in range(4):
-                each((r, c), lambda which, c=c, r=r: f_out(c, r, which).wait_send())
-        for r in range(4):
-            each((r, col), lambda which, r=r: y_out(r, which).wait_send(), crosses(r))
+            pl.when(crosses(r))(lambda r=r: whole((r, col), lambda units: await_send(y_send.at[r], units)))
         for turn in range(3):
             for way in range(2):
                 sign = 1 - 2 * way
                 r = row + sign * turn
-                each((r, col), lambda which, turn=turn, way=way: z_out(turn, way, which).wait_send(), has(r), has(row - sign))
-        each((end, far), lambda which: e_out(which).wait_send(), has(row + 1 - 2 * core))
+                pl.when(jnp.logical_and(has(r), has(row - sign)))(
+                    lambda r=r, n=2 * turn + way: whole((r, col), lambda units: await_send(z_send.at[n], units)))
+        pl.when(has(row + 1 - 2 * core))(lambda: whole((end, far), lambda units: await_send(e_send.at[0], units)))
+
+        @pl.when(row == col)
+        def _():
+            remote(red.at[pl.ds(0, 15)], red.at[pl.ds(0, 15)], t_send.at[0], t_recv.at[row], partner).wait_send()
 
     gather_drained()
-
-    quad_eye = lax.broadcasted_iota(jnp.int32, (half, half), 0) == lax.broadcasted_iota(jnp.int32, (half, half), 1)
-    trace = jnp.zeros((half, half), F32)
-    for k in range(8):
-        trace = trace + x_ref[1, k * half:(k + 1) * half, k * half:(k + 1) * half]
-    trace = jnp.where(quad_eye, trace, 0.0)
-    chem = jnp.sum(jnp.sum(trace, axis=0, keepdims=True), axis=1, keepdims=True) / order
-    occupied = jnp.full((1, 1), occ_ref[0], jnp.int32).astype(F32)
-    scale = jnp.minimum(occupied / (bounds_ref[1] - chem), (order - occupied) / (chem - bounds_ref[0])) / order
-    shift = occupied / order
-
-    def convert(n, carry):
-        i, j = n // 4, n % 4
-        low = jnp.where(i > j, half, 0)
-
-        def one(qr, qc):
-            eye = jnp.logical_and(quad_eye, i * block + qr == j * block + qc)
-            value = x_ref[1, at(i * block + qr, half), lanes(j * block + qc, half)]
-            value = scale * (jnp.where(eye, chem, 0.0) - value) + jnp.where(eye, shift, 0.0)
-            x_ref[0, at(i * block + qr, half), lanes(j * block + qc, half)] = value
-            x_ref[0, at(j * block + qc, half), lanes(i * block + qr, half)] = value.T
-
-        one(0, half)
-        one(low, low)
-
-        @pl.when(i == j)
-        def _():
-            one(half, half)
-
-        return carry
-
-    lax.fori_loop(0, 16, convert, 0)
+    stage[...] = jnp.zeros_like(stage)
 
     def sigma(flip, i):
         return i + flip * (3 - 2 * i)
@@ -274,86 +331,54 @@
             return d0 + half, d0 + half, half
         return (between if k == 2 else single)(flip, who) + (block,)
 
-    def part_copy(flip, who, k, part, slot, send, recv, where):
-        r0, c0, width = piece(flip, who, k)
-        spot = rect(slot, r0 + part * quarter, c0, quarter, width)
-        n = slot * 8 + k * 2 + part
-        return remote(spot, spot, send.at[n], recv.at[n], where)
-
     def sender(who, k):
         return who + odd * (1 - 2 * who) if k == 3 else who
 
-    def outward(k, part, slot):
-        to_row, to_col = near[part]
-        if k == 3:
-            to_col = to_col + (1 - odd) * (1 - 2 * core)
-        return part_copy(odd, core, k, part, slot, i_send, i_recv, (to_row, to_col))
-
-    def inward(k, part, slot):
-        return part_copy(1 - odd, sender(core, k), k, part, slot, i_send, i_recv, near[part])
-
-    def passed(who, k, part, slot):
-        return part_copy(1 - odd, sender(who, k), k, part, slot, w_send, w_recv, partner)
-
-    def direct(who, k, slot):
-        if k < 4:
-            r0, c0, width = piece(odd, who, k)
-        else:
-            r0, c0 = common(odd, who, k - 4)
+    def outward(k, slot):
+        r0, c0, width = piece(odd, core, k)
+        for part, (to_row, to_col) in enumerate(near):
+            if k == 3:
+                to_col = to_col + (1 - odd) * (1 - 2 * core)
+            spot = rect(slot, r0 + part * quarter, c0, quarter, width)
+            remote(spot, spot, s_send.at[slot], i_recv.at[slot * 4 + k], (to_row, to_col)).start()
+
+    def to_partner(slot, r0, c0, height, width, sem):
+        spot = rect(slot, r0, c0, height, width)
+        remote(spot, spot, s_send.at[slot], sem, partner).start()
+
+    def pair(k, r0, c0, slot, sem):
+        to_partner(slot, r0, c0, half, half if k == 1 else block, sem)
         if k == 0:
-            spots = [rect(slot, r0, c0, half, block), rect(slot, c0 + half, r0, half, half)]
-        elif k == 1:
-            spots = [rect(slot, r0, c0, half, half)]
-        else:
-            spots = [rect(slot, r0, c0, half, block), rect(slot, c0, r0, block, half)]
-        return [remote(spot, spot, d_send.at[slot * 12 + 2 * k + n], d_recv.at[slot * 12 + 2 * k + n], partner) for n, spot in enumerate(spots)]
+            to_partner(slot, c0 + half, r0, half, half, sem)
+        elif k != 1:
+            to_partner(slot, c0, r0, block, half, sem)
 
     def send_piece(k, slot):
         if k < 4:
-            for part in range(2):
-                outward(k, part, slot).start()
-        for copy in direct(core, k, slot):
-            copy.start()
+            outward(k, slot)
+            r0, c0 = piece(odd, core, k)[:2]
+        else:
+            r0, c0 = common(odd, core, k - 4)
+        pair(k, r0, c0, slot, (h_recv if k == 2 else s_recv).at[slot])
 
     def relay(k, slot):
-        for part in range(2):
-            inward(k, part, slot).wait_recv()
-            passed(core, k, part, slot).start()
-
-    def mirror(flip, who, k, slot):
-        r0, c0, _ = piece(flip, who, k)
+        await_recv(i_recv.at[slot * 4 + k], 1 if k == 1 else 2)
+        r0, c0, _ = piece(1 - odd, sender(core, k), k)
         if k == 0:
             x_ref[slot, at(c0 + half, half), lanes(r0, half)] = x_ref[slot, at(r0, half), lanes(c0 + half, half)].T
-        else:
+        elif k != 1:
             x_ref[slot, at(c0, block), lanes(r0, half)] = x_ref[slot, at(r0, half), lanes(c0, block)].T
+        pair(k, r0, c0, slot, s_recv.at[slot])
 
     def early(slot):
         relay(3, slot)
-        for copy in direct(1 - core, 2, slot):
-            copy.wait_recv()
-        mirror(1 - odd, sender(core, 3), 3, slot)
+        await_recv(h_recv.at[slot], 4)
 
     def settled(slot):
-        relay(2, slot)
-        for k in (0, 1, 3, 4, 5):
-            for copy in direct(1 - core, k, slot):
-                copy.wait_recv()
-        for k in (0, 1, 3, 2):
-            for part in range(2):
-                passed(1 - core, k, part, slot).wait_recv()
-        mirror(1 - odd, sender(1 - core, 3), 3, slot)
-        for who in range(2):
-            mirror(1 - odd, who, 0, slot)
-            mirror(1 - odd, who, 2, slot)
+        await_recv(s_recv.at[slot], 28)
 
     def drained(slot):
-        for k in range(6):
-            for copy in direct(core, k, slot):
-                copy.wait_send()
-        for k in range(4):
-            for part in range(2):
-                outward(k, part, slot).wait_send()
-                passed(core, k, part, slot).wait_send()
+        await_send(s_send.at[slot], 39)
 
     def work(u, carry):
         t, m = u // 5, u % 5
@@ -372,11 +397,16 @@
 
         @on(m == 0, t == steps - 1)
         def _():
+            relay(2, cur)
             settled(cur)
             stage[pl.ds(t, 1), :] = squares(cur)
 
         @on(m == 1, live)
         def _():
+            @pl.when(t > 0)
+            def _():
+                relay(2, cur)
+
             r0, c0, _ = piece(odd, core, 1)
             x_ref[nxt, at(r0, half), lanes(c0, half)] = product(cur, r0, c0, half, half, flag)
             send_piece(1, nxt)
@@ -470,8 +500,9 @@
                 pltpu.VMEM((2, order, order), F32),
                 pltpu.VMEM((8, 128), F32),
                 pltpu.VMEM((16, 8, 128), F32),
-                dma((18,)), dma((18,)), dma((3,)), dma((3,)), dma((12,)), dma((12,)), dma((24,)), dma((24,)),
-                dma((16,)), dma((16,)), dma((24,)), dma((24,)), dma((16,)), dma((16,)),
+                pltpu.VMEM((4, 8, 128), F32),
+                dma((1,)), dma((4,)), dma((6,)), dma((18,)), dma((1,)), dma((3,)), dma((4,)), dma((12,)), dma((1,)), dma((8,)),
+                dma((2,)), dma((8,)), dma((2,)), dma((2,)),
                 dma((15,)), dma((15,)),
                 pltpu.SemaphoreType.REGULAR((3,)),
             ],

time: 211 us -> 199 us (0.943)
  Pallas kernels: 205 us -> 193 us
    pallas_call x1, Pallas kernels: 205 us -> 193 us  [local_run(): pl.pallas_call(functools.partial(kernel, steps), out_shape=(jax.ShapeDtyp...]
where the time goes in v4:
time: 199 us
  Pallas kernels  193 us (97%)
  between operations  3.05 us (2%)
  local copies, waits for them, and re-layouts  2.78 us (1%)
    pallas_call x1, Pallas kernels, local_run(): pl.pallas_call(functools.partial(kernel, steps), out_shape=(jax.ShapeDtyp...  193 us

profile of v4, /device:TPU:0, one launch (start us, length us, event | category | flops | bytes accessed | tf_op | source)
XLA Modules:
  0.0 199.0 jit_solution(9425962683771655841)
XLA Ops:
  1.3 193.1 %shard_map.67 = (f32[512,512]{1,0:T(8,128)}, f32[6]{0:T(128)}, f32[1]{0:T(128)}) custom-call(f32[512,512]{1,0:T(8,128)} %h_ref.1, f32[2]{0:T(128)} %bounds_ref.1, s32[1]{0:T(128)S(6)} %copy.10.occ_ref, s32[6]{0:T(128)} %flag_ref.1), custom_call_target="tpu_custom_call" | custom-call | tf_op jit(solution)/shard_map/pallas_call | solution.py:490
  194.4 0.0 copy-start
  194.4 2.3 %copy.11 = f32[512,512]{1,0:T(8,128)} copy(f32[512,512]{1,0:T(8,128)} %get-tuple-element.6) | data formatting | bytes 2097152
  196.7 0.0 copy-done
  196.7 0.5 copy.12
Async XLA Ops:
  194.4 2.3 %copy-start = (f32[6]{0:T(128)S(1)}, f32[6]{0:T(128)}, u32[]{:S(2)}) copy-start(f32[6]{0:T(128)} %get-tuple-element.7) | copy-start | bytes 76

commit v5 on v4

--- a/solution.py
+++ b/solution.py
@@ -16,7 +16,7 @@
     return row, (col + 2) % 4
 
 
-def kernel(steps, h_ref, bounds_ref, occ_ref, flag_ref, dens_ref, occs_ref, energy_ref, x_ref, stage, red, traces, t_send, t_recv, z_send, z_recv, e_send,
+def kernel(steps, h_hbm, bounds_ref, occ_ref, flag_ref, dens_hbm, occs_ref, energy_ref, h_ref, io_sem, x_ref, stage, red, traces, t_send, t_recv, z_send, z_recv, e_send,
            e_recv, y_send, y_recv, f_send, f_recv, s_send, i_recv, h_recv, s_recv, r_send, r_recv, credit):
     block = h_ref.shape[0]
     half = block // 2
@@ -37,12 +37,16 @@
             src_ref=src, dst_ref=dst, send_sem=send, recv_sem=recv, device_id=(spin,) + tuple(where), device_id_type=pl.DeviceIdType.MESH
         )
 
+    load = pltpu.make_async_copy(h_hbm, h_ref, io_sem.at[0])
+    load.start()
+
     others = [(dr, dc) for dr in range(4) for dc in range(4) if dr or dc]
     barrier = pltpu.get_barrier_semaphore()
     for dr, dc in others:
         pl.semaphore_signal(
             barrier, inc=1, device_id=(spin, (row + dr) % 4, (col + dc) % 4), device_id_type=pl.DeviceIdType.MESH
         )
+    load.wait()
     pl.semaphore_wait(barrier, len(others))
 
     def await_send(sem, units):
@@ -363,22 +367,27 @@
 
     def relay(k, slot):
         await_recv(i_recv.at[slot * 4 + k], 1 if k == 1 else 2)
-        r0, c0, _ = piece(1 - odd, sender(core, k), k)
+        r0, c0, width = piece(1 - odd, sender(core, k), k)
+        to_partner(slot, r0, c0, half, width, s_recv.at[slot])
         if k == 0:
             x_ref[slot, at(c0 + half, half), lanes(r0, half)] = x_ref[slot, at(r0, half), lanes(c0 + half, half)].T
+            to_partner(slot, c0 + half, r0, half, half, s_recv.at[slot])
         elif k != 1:
             x_ref[slot, at(c0, block), lanes(r0, half)] = x_ref[slot, at(r0, half), lanes(c0, block)].T
-        pair(k, r0, c0, slot, s_recv.at[slot])
+            if k == 3:
+                to_partner(slot, c0, r0, block, half, s_recv.at[slot])
 
     def early(slot):
         relay(3, slot)
         await_recv(h_recv.at[slot], 4)
 
     def settled(slot):
-        await_recv(s_recv.at[slot], 28)
+        await_recv(s_recv.at[slot], 26)
+        r0, c0, _ = piece(1 - odd, 1 - core, 2)
+        x_ref[slot, at(c0, block), lanes(r0, half)] = x_ref[slot, at(r0, half), lanes(c0, block)].T
 
     def drained(slot):
-        await_send(s_send.at[slot], 39)
+        await_send(s_send.at[slot], 37)
 
     def work(u, carry):
         t, m = u // 5, u % 5
@@ -460,8 +469,9 @@
     last = (steps - 1) % 2
 
     final = x_ref[1 - last, at(row * block, block), lanes(col * block, block)]
-    dens_ref[...] = final
     stage[steps:steps + 1, :] = lane_sums(final * h_ref[...])
+    store = pltpu.make_async_copy(x_ref.at[1 - last, at(row * block, block), lanes(col * block, block)], dens_hbm, io_sem.at[1])
+    store.start()
     drained(last)
 
     red[row * 4 + col] = stage[...]
@@ -478,6 +488,7 @@
     energy_ref[0] = 2.0 * jnp.sum(total[steps:steps + 1, :])
     for n, (dr, dc) in enumerate(others):
         remote(stage, red.at[row * 4 + col], r_send.at[n], r_recv.at[n], ((row + dr) % 4, (col + dc) % 4)).wait_send()
+    store.wait()
 
 
 def solution(mesh):
@@ -485,7 +496,7 @@
         block, steps = ham_block.shape[0], branches.shape[0]
         order = 4 * block
         dma = pltpu.SemaphoreType.DMA
-        vmem = pl.BlockSpec(memory_space=pltpu.VMEM)
+        hbm = pl.BlockSpec(memory_space=pl.ANY)
         smem = pl.BlockSpec(memory_space=pltpu.SMEM)
         return pl.pallas_call(
             functools.partial(kernel, steps),
@@ -494,9 +505,11 @@
                 jax.ShapeDtypeStruct((steps,), F32),
                 jax.ShapeDtypeStruct((1,), F32),
             ),
-            in_specs=[vmem, smem, smem, smem],
-            out_specs=(vmem, smem, smem),
+            in_specs=[hbm, smem, smem, smem],
+            out_specs=(hbm, smem, smem),
             scratch_shapes=[
+                pltpu.VMEM((block, block), F32),
+                dma((2,)),
                 pltpu.VMEM((2, order, order), F32),
                 pltpu.VMEM((8, 128), F32),
                 pltpu.VMEM((16, 8, 128), F32),

time: 199 us -> 196 us (0.985)
  Pallas kernels: 193 us -> 189 us
    pallas_call x1, Pallas kernels: 193 us -> 189 us  [local_run(): pl.pallas_call(functools.partial(kernel, steps), out_shape=(jax.ShapeDtyp...]
where the time goes in v5:
time: 196 us; the launch traced here: 195 us
  Pallas kernels  189 us (96%)
  between operations  3.05 us (2%)
  local copies, waits for them, and re-layouts  2.78 us (1%)
    pallas_call x1, Pallas kernels, local_run(): pl.pallas_call(functools.partial(kernel, steps), out_shape=(jax.ShapeDtyp...  189 us

profile of v5, /device:TPU:0, one launch (start us, length us, event | category | flops | bytes accessed | tf_op | source)
XLA Modules:
  0.0 195.3 jit_solution(8167845703178509863)
XLA Ops:
  1.3 189.5 %shard_map.67 = (f32[512,512]{1,0:T(8,128)}, f32[6]{0:T(128)}, f32[1]{0:T(128)}) custom-call(f32[512,512]{1,0:T(8,128)} %h_hbm.1, f32[2]{0:T(128)} %bounds_ref.1, s32[1]{0:T(128)S(6)} %copy.10.occ_ref, s32[6]{0:T(128)} %flag_ref.1), custom_call_target="tpu_custom_call" | custom-call | tf_op jit(solution)/shard_map/pallas_call | solution.py:501
  190.8 0.0 copy-start
  190.8 2.3 %copy.11 = f32[512,512]{1,0:T(8,128)} copy(f32[512,512]{1,0:T(8,128)} %get-tuple-element.6) | data formatting | bytes 2097152
  193.1 0.0 copy-done
  193.1 0.5 copy.12
Async XLA Ops:
  190.8 2.3 %copy-start = (f32[6]{0:T(128)S(1)}, f32[6]{0:T(128)}, u32[]{:S(2)}) copy-start(f32[6]{0:T(128)} %get-tuple-element.7) | copy-start | bytes 76
